TPU v7x, 256 devices: a whole 4x4x8 slice. The times are simulated.
256 devices in a mesh: outer: 8 (over x, y_hi), inner: 32 (over y_lo, z, core).
Axes of the slice: x: 4, y: 4 (y_hi: 2, y_lo: 2; y = y_hi * 2 + y_lo), z: 8, core: 2. Of those that a mesh axis runs over, the one named last changes fastest.
Arguments:
- tokens: bfloat16 [32768, 4096], P('inner', 'outer'), may hold values from -6 to 6
- cotangent: bfloat16 [32768, 4096], P('inner', 'outer'), may hold values from -0.03125 to 0.03125
- weight_cache: bfloat16 [4096, 4096], P(None, 'outer'), may hold values from -0.09375 to 0.09375
- weight_delta: bfloat16 [4096, 4096], P('inner', 'outer'), may hold values from -0.078125 to 0.078125
- sign_bits: int32 [4096], P('outer'), may hold values from 0 to 1
- master: float32 [4096, 4096], P('inner', 'outer'), may hold values from -1.5 to 1.5
- moment: float32 [4096, 4096], P('inner', 'outer'), may hold values from -6 to 6
- variance: float32 [4096, 4096], P('inner', 'outer'), may hold values from 0.25 to 4
Outputs:
- activation: float32 [32768, 4096], P('inner', 'outer')
- new_master: float32 [4096, 4096], P('inner', 'outer')
- new_moment: float32 [4096, 4096], P('inner', 'outer')
- new_variance: float32 [4096, 4096], P('inner', 'outer')
- block_scales: float32 [4096, 32], P('inner', 'outer')
All inputs are finite; a program needn't handle non-finite values.
Results may differ from a plain program's by a relative error of at most 0.003.
Values may be sent and summed in bfloat16 or wider, within the bound.
A program may use at most 128 MiB of HBM per device.

v0:
```python
import jax
import jax.numpy as jnp
from jax import lax
from jax.sharding import Mesh
from jax.sharding import PartitionSpec as P

BLOCK = 128
INNER = ("inner_0", "inner_1", "inner_2")


def split_up(value, dim, devices):
    before, after = (value.shape[:dim], value.shape[dim + 1 :])
    return jnp.moveaxis(value.reshape(*before, devices, -1, *after), dim, 0)


def summed_rows(value, chips, core, dim):
    sizes = (lax.axis_size(chips), lax.axis_size(core))
    blocks = split_up(value, dim, sizes[0] * sizes[1])
    inside = blocks.shape[1:]
    blocks = blocks.reshape(*sizes, *inside).swapaxes(0, 1).reshape(-1, *inside)
    blocks = lax.psum_scatter(blocks, core, scatter_dimension=0, tiled=True)
    return lax.psum_scatter(blocks, chips, scatter_dimension=0, tiled=True)[0]


def hadamard_table(length):
    first = jnp.arange(length, dtype=jnp.int32)[:, None]
    second = jnp.arange(length, dtype=jnp.int32)[None, :]
    common = jnp.bitwise_and(first, second)
    parity = jnp.zeros((length, length), jnp.int32)
    for place in range(length.bit_length() - 1):
        parity = parity + jnp.bitwise_and(jnp.right_shift(common, place), 1)
    return (1 - 2 * (parity % 2)).astype(jnp.float32) / jnp.sqrt(jnp.float32(length))


def smooth(values, signs, table):
    height = values.shape[0]
    blocks = values.reshape(height, -1, table.shape[0]) * signs.reshape(-1, table.shape[0])
    mixed = jnp.einsum("rbk,kj->rbj", blocks, table, precision=lax.Precision.HIGHEST)
    return mixed.reshape(height, -1)


def unsmooth(values, signs, table):
    height = values.shape[0]
    blocks = values.reshape(height, -1, table.shape[0])
    mixed = jnp.einsum("rbj,jk->rbk", blocks, table, precision=lax.Precision.HIGHEST)
    return (mixed * signs.reshape(-1, table.shape[0])).reshape(height, -1)


def outer_product(left, right):
    return lax.dot_general(
        left, right, (((0,), (0,)), ((), ())), preferred_element_type=jnp.float32
    )


def body(tokens, cotangent, weight_cache, weight_delta, sign_bits, master, moment, variance):
    table = hadamard_table(BLOCK)
    signs = (1 - 2 * sign_bits).astype(jnp.float32)
    shard_rows = master.shape[0]
    gathered = lax.all_gather(tokens, "outer", axis=1, tiled=True)
    merged = (
        weight_cache.astype(jnp.float32)
        + lax.all_gather(weight_delta, INNER, axis=0, tiled=True).astype(jnp.float32)
    ).astype(jnp.bfloat16)
    columns = gathered
    output = jnp.dot(columns, merged, preferred_element_type=jnp.float32)
    columns = gathered
    partial_value = outer_product(columns, cotangent)
    summed = summed_rows(partial_value, ("inner_0", "inner_1"), "inner_2", 0)
    smoothed = smooth(summed, signs, table)
    block_scales = jnp.max(jnp.abs(smoothed.reshape(shard_rows, -1, BLOCK)), axis=2)
    restored = unsmooth(smoothed, signs, table)
    new_moment = 0.9 * moment + 0.1 * restored
    new_variance = 0.95 * variance + 0.05 * restored * restored
    corrected = new_moment / (1.0 - 0.9**10)
    spread = jnp.sqrt(new_variance / (1.0 - 0.95**10)) + 1e-08
    new_master = master - 0.01 * (corrected / spread + 0.1 * master)
    return (output, new_master, new_moment, new_variance, block_scales)


def solution(mesh):
    torus = Mesh(
        mesh.devices.reshape(mesh.shape["outer"], 2, 8, 2),
        ("outer", "inner_0", "inner_1", "inner_2"),
    )
    in_specs = (
        P(INNER, "outer"),
        P(INNER, "outer"),
        P(None, "outer"),
        P(INNER, "outer"),
        P("outer"),
        P(INNER, "outer"),
        P(INNER, "outer"),
        P(INNER, "outer"),
    )
    out_specs = (
        P(INNER, "outer"),
        P(INNER, "outer"),
        P(INNER, "outer"),
        P(INNER, "outer"),
        P(INNER, "outer"),
    )
    return jax.shard_map(body, mesh=torus, in_specs=in_specs, out_specs=out_specs, check_vma=False)
```

profile of v0, /device:TPU:56, one launch (start us, length us, event | category | flops | bytes accessed | tf_op | source)
XLA Modules:
  0.0 265.0 jit_solution(17581240308026730228)
XLA Ops:
  8.0 0.0 copy-start
  8.0 0.0 all-gather.5.cloned.1.call-start
  8.1 0.7 all-gather.5.cloned.1.call-update
  8.7 0.0 reduce-scatter.3.cloned.1.call-start
  8.8 127.8 %all-gather.5.cloned.1.call-done = bf16[1024,4096]{1,0:T(8,128)(2,1)} async-done(((bf16[1024,512]{1,0:T(8,128)(2,1)}), bf16[1024,4096]{1,0:T(8,128)(2,1)}) %all-gather.5.cloned.1.call-update) | async-done | bytes 8388624 | tf_op jit(solution)/shard_map/all_gather | solution.py:59
  136.6 0.0 copy-done
  136.6 7.1 %fusion.47 = f32[4096,512]{1,0:T(8,128)S(1)} fusion(bf16[1024,4096]{1,0:T(8,128)(2,1)} %all-gather.5.cloned.1.call-done, bf16[1024,512]{1,0:T(8,128)(2,1)S(1)} %copy-done), kind=kOutput, calls=%fused_computation.54 | convolution fusion | flops 4294967296 | bytes 17825792 | tf_op jit(solution)/shard_map/dot_general | solution.py:50
  143.8 4.2 %copy.19 = f32[16,2,128,512]{3,2,0,1:T(8,128)} copy(f32[16,2,128,512]{3,2,1,0:T(8,128)S(1)} %bitcast.21) | data formatting | bytes 16777216 | tf_op jit(solution)/shard_map/reshape;reshape | solution.py:20
  148.0 0.0 copy-start.2
  148.0 0.0 reduce-scatter.3.cloned.1.call-update
  148.1 0.0 all-gather.3.cloned.1.call-start
  148.1 0.5 all-gather.3.cloned.1.call-update
  148.6 0.0 reduce-scatter.5.cloned.1.call-start
  148.7 21.8 %reduce-scatter.3.cloned.1.call-done = f32[16,128,512]{2,1,0:T(8,128)} async-done(((f32[32,128,512]{2,1,0:T(8,128)}), f32[16,128,512]{2,1,0:T(8,128)}) %reduce-scatter.3.cloned.1.call-update) | async-done | bytes 4194320 | tf_op jit(solution)/shard_map/reduce_scatter | solution.py:21
  170.5 0.0 reduce-scatter.5.cloned.1.call-update
  170.5 0.0 copy-done.2
  170.5 0.0 copy-start.1
  170.5 57.3 %all-gather.3.cloned.1.call-done = bf16[4096,512]{1,0:T(8,128)(2,1)} async-done(((bf16[128,512]{1,0:T(8,128)(2,1)}), bf16[4096,512]{1,0:T(8,128)(2,1)}) %all-gather.3.cloned.1.call-update) | async-done | bytes 4194320 | tf_op jit(solution)/shard_map/all_gather | solution.py:62
  227.8 9.6 %fusion.1 = f32[1024,512]{0,1:T(8,128)S(1)} fusion(bf16[1024,4096]{1,0:T(8,128)(2,1)} %all-gather.5.cloned.1.call-done, bf16[4096,512]{1,0:T(8,128)(2,1)} %all-gather.3.cloned.1.call-done, bf16[4096,512]{1,0:T(8,128)(2,1)} %param.10), kind=kOutput, calls=%fused_computation.2 | convolution fusion | flops 4303355904 | bytes 18874368 | tf_op jit(solution)/shard_map/dot_general | solution.py:65
  237.4 1.8 copy.26
  239.2 13.8 %reduce-scatter.5.cloned.1.call-done = f32[1,128,512]{2,1,0:T(8,128)} async-done(((f32[16,128,512]{2,1,0:T(8,128)}), f32[1,128,512]{2,1,0:T(8,128)}) %reduce-scatter.5.cloned.1.call-update) | async-done | bytes 262160 | tf_op jit(solution)/shard_map/reduce_scatter | solution.py:22
  253.1 1.1 copy.20
  254.1 1.1 abs_reduce_fusion
  255.2 0.4 convolution_multiply_fusion
  255.7 0.1 copy.23
  255.8 0.0 copy-done.1
  255.8 2.0 multiply_subtract_fusion
  (1 shorter events, 0.0 us)
Async XLA Ops:
  8.0 128.6 %copy-start = (bf16[1024,512]{1,0:T(8,128)(2,1)S(1)}, bf16[1024,512]{1,0:T(8,128)(2,1)}, u32[]{:S(2)}) copy-start(bf16[1024,512]{1,0:T(8,128)(2,1)} %param.9) | copy-start | bytes 3145732
  8.0 128.6 %all-gather.5.cloned.1.call-start = ((), (), s32[]{:S(2)}) async-start(), calls=%async_computation.3 | async-start | bytes 9437184 | tf_op jit(solution)/shard_map/all_gather | solution.py:59
  8.7 161.7 %reduce-scatter.3.cloned.1.call-start = ((), (), s32[]{:S(2)}) async-start(), calls=%async_computation.4 | async-start | bytes 12582912 | tf_op jit(solution)/shard_map/reduce_scatter | solution.py:21
  148.0 22.5 %copy-start.2 = (s32[512]{0:T(512)S(1)}, s32[512]{0:T(512)}, u32[]{:S(2)}) copy-start(s32[512]{0:T(512)} %param.12) | copy-start | bytes 6148
  148.1 79.8 %all-gather.3.cloned.1.call-start = ((), (), s32[]{:S(2)}) async-start(), calls=%async_computation.2 | async-start | bytes 4325376 | tf_op jit(solution)/shard_map/all_gather | solution.py:62
  148.6 104.4 %reduce-scatter.5.cloned.1.call-start = ((), (), s32[]{:S(2)}) async-start(), calls=%async_computation.5 | async-start | bytes 4456448 | tf_op jit(solution)/shard_map/reduce_scatter | solution.py:22
  170.5 85.3 %copy-start.1 = (f32[128,512]{1,0:T(8,128)S(1)}, f32[128,512]{1,0:T(8,128)}, u32[]{:S(2)}) copy-start(f32[128,512]{1,0:T(8,128)} %param.13) | copy-start | bytes 786436
Sparse Core Ops, SparseCore 0:
  11.3 125.2 all-gather.4
  148.2 22.2 reduce-scatter.2
  173.0 79.9 reduce-scatter.4
Sparse Core Ops, SparseCore 1:
  150.4 77.4 all-gather.2
where the time goes:
time: 268 us; the launch traced here: 265 us
  waiting for transfers between devices  222 us (83%)
  matrix products  18.2 us (7%)
  between operations  15.3 us (6%)
  local copies, waits for them, and re-layouts  7.28 us (3%)
    all_gather x1, waiting for transfers between devices, body(): gathered = lax.all_gather(tokens, 'outer', axis=1, tiled=True)  128 us
    all_gather x1, waiting for transfers between devices, body(): lax.all_gather(weight_delta, INNER, axis=0, tiled=True).astype(jnp.float32)  57.3 us
    reduce_scatter x1, waiting for transfers between devices, summed_rows(): blocks = lax.psum_scatter(blocks, core, scatter_dimension=0, tiled=True)  21.8 us
    reduce_scatter x1, waiting for transfers between devices, summed_rows(): return lax.psum_scatter(blocks, chips, scatter_dimension=0, tiled=True)[0]  13.8 us
    dot_general x1, matrix products, body(): output = jnp.dot(columns, merged, preferred_element_type=jnp.float32)  9.55 us
    dot_general x1, matrix products, outer_product(): lax.dot_general(left, right, (((0,), (0,)), ((), ())), preferred_element_...  7.12 us
  transfers between devices with their start and end apart: 4, of which 4 were waited for; matrix products, arithmetic and copies ran while one was open for 4% of the time, Pallas kernels for 0%

commit v1 on v0

v1 whole, which is shorter than its diff:
```python
import functools

import jax
import jax.numpy as jnp
import numpy as np
from jax import lax
from jax.experimental import pallas as pl
from jax.experimental.pallas import tpu as pltpu
from jax.sharding import Mesh
from jax.sharding import PartitionSpec as P

BLOCK = 128
OUTER = ("x", "yh")
INNER = ("yl", "z", "c")
NX, NZ = 4, 8
HALF = 256
MESH = pl.DeviceIdType.MESH
F32, BF16 = jnp.float32, jnp.bfloat16


def transport(
    tokens, cotangent, cache, delta,
    act, grad,
    tok, cot, cot_t, weight, dbuf, gbuf, grcv, zsnd, zrcv, zloc, ysnd, yrcv,
    load_sem, tok_send, tok_recv, d2d_send, d2d_recv, z_send, z_recv, y_send, y_recv,
    dy_sem, dz_send, dz_recv, dc_send, dc_recv,
):
    x, yh, yl = lax.axis_index("x"), lax.axis_index("yh"), lax.axis_index("yl")
    z, c = lax.axis_index("z"), lax.axis_index("c")
    right, left = {"x": (x + 1) % NX}, {"x": (x + 3) % NX}
    across, beside, sibling = {"yh": 1 - yh}, {"yl": 1 - yl}, {"c": 1 - c}
    up, down = {"z": (z + 1) % NZ}, {"z": (z + 7) % NZ}

    def slot(dx, dy, half):
        row = yh if dy == 0 else 1 - yh
        return 4 * ((x + dx) % NX) + 2 * row + half

    own_a, own_b = slot(0, 0, 0), slot(0, 0, 1)
    l_a, l_b, r_a, r_b = slot(3, 0, 0), slot(3, 0, 1), slot(1, 0, 0), slot(1, 0, 1)
    ll_a, ll_b = slot(2, 0, 0), slot(2, 0, 1)
    p_a, p_b = slot(0, 1, 0), slot(0, 1, 1)
    pl_a, pl_b, pr_a, pr_b = slot(3, 1, 0), slot(3, 1, 1), slot(1, 1, 0), slot(1, 1, 1)
    pll_a, pll_b = slot(2, 1, 0), slot(2, 1, 1)

    load_a = pltpu.make_async_copy(tokens.at[:, pl.ds(0, HALF)], tok.at[own_a], load_sem.at[0])
    load_b = pltpu.make_async_copy(tokens.at[:, pl.ds(HALF, HALF)], tok.at[own_b], load_sem.at[1])
    load_cot = pltpu.make_async_copy(cotangent, cot, load_sem.at[2])
    load_delta = pltpu.make_async_copy(delta, dbuf.at[z, c, yl], load_sem.at[3])
    load_cache = pltpu.make_async_copy(cache, weight, load_sem.at[4])
    for copy in (load_a, load_b, load_cot, load_delta, load_cache):
        copy.start()

    barrier = pltpu.get_barrier_semaphore()
    peers = [right, left, across, beside, sibling]
    peers += [{"z": (z + step) % NZ} for step in range(1, NZ)]
    for peer in peers:
        pl.semaphore_signal(barrier, inc=1, device_id=peer, device_id_type=MESH)
    pl.semaphore_wait(barrier, len(peers))

    way = {"right": (0, right), "left": (1, left), "across": (2, across)}

    def token_copy(place, direction):
        lane, peer = way[direction]
        return pltpu.make_async_remote_copy(
            src_ref=tok.at[place], dst_ref=tok.at[place],
            send_sem=tok_send.at[lane, place], recv_sem=tok_recv.at[place],
            device_id=peer, device_id_type=MESH,
        )

    sent = []

    def send(place, direction):
        token_copy(place, direction).start()
        sent.append((place, direction))

    def arrived(place):
        token_copy(place, "right").wait_recv()

    def d2d_copy(place):
        return pltpu.make_async_remote_copy(
            src_ref=gbuf.at[place, 1 - c], dst_ref=grcv.at[place],
            send_sem=d2d_send.at[place], recv_sem=d2d_recv.at[place],
            device_id=sibling, device_id_type=MESH,
        )

    def target(place):
        block = place // 2
        return block // 4, 2 * (block % 4) + place % 2

    def z_copy(place):
        rows, depth = target(place)
        return pltpu.make_async_remote_copy(
            src_ref=zsnd.at[place], dst_ref=zrcv.at[rows, z],
            send_sem=z_send.at[place], recv_sem=z_recv.at[rows, z],
            device_id={"z": depth}, device_id_type=MESH,
        )

    def pick(places, i):
        value = places[0]
        for k in range(1, len(places)):
            value = jnp.where(i == k, places[k], value)
        return value

    def gradients(*places):
        def product(i, carry):
            place = pick(places, i)
            terms = jnp.dot(cot_t[...], tok[place], preferred_element_type=F32)
            gbuf[place, 0] = terms[:, :BLOCK]
            gbuf[place, 1] = terms[:, BLOCK:]
            d2d_copy(place).start()
            return carry

        def merge(i, carry):
            place = pick(places, i)
            d2d_copy(place).wait_recv()
            total = gbuf[place, c] + grcv[place]
            zsnd[place] = total.astype(BF16)
            rows, depth = target(place)

            @pl.when(depth != z)
            def _():
                z_copy(place).start()

            @pl.when(depth == z)
            def _():
                zloc[rows] = total

            return carry

        lax.fori_loop(0, len(places), product, 0)
        lax.fori_loop(0, len(places), merge, 0)

    def dz_copy(origin, lane, peer):
        return pltpu.make_async_remote_copy(
            src_ref=dbuf.at[origin, c], dst_ref=dbuf.at[origin, c],
            send_sem=dz_send.at[lane, origin], recv_sem=dz_recv.at[origin],
            device_id=peer, device_id_type=MESH,
        )

    def dc_copy(origin):
        return pltpu.make_async_remote_copy(
            src_ref=dbuf.at[origin, c], dst_ref=dbuf.at[origin, c],
            send_sem=dc_send.at[origin], recv_sem=dc_recv.at[origin],
            device_id=sibling, device_id_type=MESH,
        )

    dy_copy = pltpu.make_async_remote_copy(
        src_ref=dbuf.at[z, c, yl], dst_ref=dbuf.at[z, c, yl],
        send_sem=dy_sem.at[0], recv_sem=dy_sem.at[1],
        device_id=beside, device_id_type=MESH,
    )
    dy_in = pltpu.make_async_remote_copy(
        src_ref=dbuf.at[z, c, 1 - yl], dst_ref=dbuf.at[z, c, 1 - yl],
        send_sem=dy_sem.at[0], recv_sem=dy_sem.at[1],
        device_id=beside, device_id_type=MESH,
    )
    dz_sent = []

    def delta_step(step):
        below, above = (z + NZ - step) % NZ, (z + step) % NZ
        if step == 0:
            dy_in.wait_recv()
        else:
            dz_copy(below, 0, up).wait_recv()
        if step < 4:
            dz_copy(below, 0, up).start()
            dz_sent.append((below, 0, up))
        dc_copy(below).start()
        if 0 < step < 4:
            dz_copy(above, 1, down).wait_recv()
        if step < 3:
            dz_copy(above, 1, down).start()
            dz_sent.append((above, 1, down))
        if 0 < step < 4:
            dc_copy(above).start()

    load_a.wait()
    send(own_a, "right")
    send(own_a, "across")
    load_b.wait()
    send(own_b, "left")
    send(own_b, "right")
    send(own_a, "left")
    send(own_b, "across")
    load_delta.wait()
    dy_copy.start()
    load_cot.wait()
    cot_t[...] = cot[...].T
    gradients(own_a, own_b)
    delta_step(0)

    arrived(l_a)
    send(l_a, "right")
    send(l_a, "across")
    arrived(r_b)
    send(r_b, "left")
    send(r_b, "across")
    arrived(p_a)
    send(p_a, "left")
    gradients(l_a, r_b, p_a)
    delta_step(1)

    arrived(l_b)
    arrived(r_a)
    arrived(p_b)
    gradients(l_b, r_a, p_b)
    delta_step(2)

    arrived(pl_a)
    send(pl_a, "right")
    send(p_b, "right")
    arrived(ll_a)
    arrived(ll_b)
    gradients(ll_a, ll_b, pl_a)
    delta_step(3)

    arrived(pr_b)
    send(pr_b, "left")
    arrived(pr_a)
    arrived(pll_a)
    gradients(pr_a, pr_b, pll_a)
    delta_step(4)

    load_cache.wait()
    for origin in range(NZ):
        pltpu.make_async_remote_copy(
            src_ref=dbuf.at[origin, 1 - c], dst_ref=dbuf.at[origin, 1 - c],
            send_sem=dc_send.at[origin], recv_sem=dc_recv.at[origin],
            device_id=sibling, device_id_type=MESH,
        ).wait_recv()

    def rebuild(j, carry):
        rows = pl.ds(pl.multiple_of(j * BLOCK, BLOCK), BLOCK)
        change = dbuf[(j % 16) // 2, j % 2, j // 16]
        weight[rows, :] = (weight[rows, :].astype(F32) + change.astype(F32)).astype(BF16)
        return carry

    lax.fori_loop(0, 32, rebuild, 0)

    arrived(pl_b)
    arrived(pll_b)
    gradients(pl_b, pll_b)

    act[...] = jnp.zeros_like(act)

    def project(k, carry):
        first = pl.ds(pl.multiple_of(2 * k * HALF, HALF), HALF)
        second = pl.ds(pl.multiple_of((2 * k + 1) * HALF, HALF), HALF)
        terms = jnp.dot(tok[2 * k], weight[first, :], preferred_element_type=F32)
        terms += jnp.dot(tok[2 * k + 1], weight[second, :], preferred_element_type=F32)
        act[...] += terms
        return carry

    lax.fori_loop(0, 8, project, 0)

    def collected(rows):
        total = zloc[rows]
        for step in range(1, NZ):
            source = (z + step) % NZ
            pltpu.make_async_remote_copy(
                src_ref=zrcv.at[rows, source], dst_ref=zrcv.at[rows, source],
                send_sem=z_send.at[0], recv_sem=z_recv.at[rows, source],
                device_id={"z": source}, device_id_type=MESH,
            ).wait_recv()
            total = total + zrcv[rows, source].astype(F32)
        return total

    ysnd[...] = collected(1 - yl).astype(BF16)
    y_copy = pltpu.make_async_remote_copy(
        src_ref=ysnd, dst_ref=yrcv, send_sem=y_send, recv_sem=y_recv,
        device_id=beside, device_id_type=MESH,
    )
    y_copy.start()
    grad[...] = collected(yl)
    y_copy.wait_recv()
    grad[...] += yrcv[...].astype(F32)

    y_copy.wait_send()
    dy_copy.wait_send()
    for place, direction in sent:
        token_copy(place, direction).wait_send()
    for origin, lane, peer in dz_sent:
        dz_copy(origin, lane, peer).wait_send()

    def drain_delta(origin, carry):
        dc_copy(origin).wait_send()
        return carry

    def drain(place, carry):
        d2d_copy(place).wait_send()

        @pl.when(target(place)[1] != z)
        def _():
            z_copy(place).wait_send()

        return carry

    lax.fori_loop(0, NZ, drain_delta, 0)
    lax.fori_loop(0, 16, drain, 0)


def hadamard(length):
    first = lax.broadcasted_iota(jnp.int32, (length, length), 0)
    second = lax.broadcasted_iota(jnp.int32, (length, length), 1)
    common = jnp.bitwise_and(first, second)
    parity = jnp.zeros((length, length), jnp.int32)
    for place in range(length.bit_length() - 1):
        parity = parity + jnp.bitwise_and(jnp.right_shift(common, place), 1)
    signs = (1 - 2 * jnp.bitwise_and(parity, 1)).astype(F32)
    return signs / np.sqrt(np.float32(length))


def update(
    act_in, grad_t, sign_bits, master, moment, variance,
    act, new_master, new_moment, new_variance, scales,
    held, sem,
):
    fetch = pltpu.make_async_copy(act_in, held, sem.at[0])
    fetch.start()
    table = hadamard(BLOCK)
    fetch.wait()
    store = pltpu.make_async_copy(held, act, sem.at[1])
    store.start()
    for k in range(master.shape[1] // BLOCK):
        span = pl.ds(k * BLOCK, BLOCK)
        signs = (1 - 2 * sign_bits[:, span]).astype(F32)
        gradient = grad_t[span, :].T
        smoothed = jnp.dot(
            gradient * signs, table, precision=lax.Precision.HIGHEST, preferred_element_type=F32
        )
        scales[:, pl.ds(k, 1)] = jnp.max(jnp.abs(smoothed), axis=1, keepdims=True)
        restored = signs * jnp.dot(
            smoothed, table, precision=lax.Precision.HIGHEST, preferred_element_type=F32
        )
        first = 0.9 * moment[:, span] + 0.1 * restored
        second = 0.95 * variance[:, span] + 0.05 * restored * restored
        corrected = first / (1.0 - 0.9**10)
        spread = jnp.sqrt(second / (1.0 - 0.95**10)) + 1e-08
        old = master[:, span]
        new_moment[:, span] = first
        new_variance[:, span] = second
        new_master[:, span] = old - 0.01 * (corrected / spread + 0.1 * old)
    store.wait()


def body(tokens, cotangent, weight_cache, weight_delta, sign_bits, master, moment, variance):
    count, width = tokens.shape
    columns = cotangent.shape[1]
    inside = pl.BlockSpec(memory_space=pltpu.VMEM)
    outside = pl.BlockSpec(memory_space=pl.ANY)
    dma = pltpu.SemaphoreType.DMA
    piece = (columns, BLOCK)
    act, grad_t = pl.pallas_call(
        transport,
        out_shape=(
            jax.ShapeDtypeStruct((count, columns), F32),
            jax.ShapeDtypeStruct(piece, F32),
        ),
        in_specs=[outside] * 4,
        out_specs=(inside, inside),
        scratch_shapes=[
            pltpu.VMEM((16, count, HALF), BF16),
            pltpu.VMEM((count, columns), BF16),
            pltpu.VMEM((columns, count), BF16),
            pltpu.VMEM(weight_cache.shape, BF16),
            pltpu.VMEM((NZ, 2, 2, BLOCK, columns), BF16),
            pltpu.VMEM((16, 2, *piece), F32),
            pltpu.VMEM((16, *piece), F32),
            pltpu.VMEM((16, *piece), BF16),
            pltpu.VMEM((2, NZ, *piece), BF16),
            pltpu.VMEM((2, *piece), F32),
            pltpu.VMEM(piece, BF16),
            pltpu.VMEM(piece, BF16),
            dma((5,)), dma((3, 16)), dma((16,)), dma((16,)), dma((16,)), dma((16,)),
            dma((2, NZ)), dma, dma, dma((2,)), dma((2, NZ)), dma((NZ,)), dma((NZ,)), dma((NZ,)),
        ],
        compiler_params=pltpu.CompilerParams(
            collective_id=0, has_side_effects=True, vmem_limit_bytes=58 * 2**20
        ),
        name="transport",
    )(tokens, cotangent, weight_cache, weight_delta)
    small = jax.ShapeDtypeStruct(master.shape, F32)
    act, new_master, new_moment, new_variance, scales = pl.pallas_call(
        update,
        out_shape=(
            jax.ShapeDtypeStruct((count, columns), F32),
            small, small, small,
            jax.ShapeDtypeStruct((master.shape[0], columns // BLOCK), F32),
        ),
        in_specs=[outside] + [inside] * 5,
        out_specs=(outside, inside, inside, inside, inside),
        scratch_shapes=[pltpu.VMEM((count, columns), F32), dma((2,))],
        name="update",
    )(act, grad_t, sign_bits.reshape(1, columns), master, moment, variance)
    return act, new_master, new_moment, new_variance, scales


def solution(mesh):
    torus = Mesh(mesh.devices.reshape(NX, 2, 2, NZ, 2), OUTER + INNER)
    split = P(INNER, OUTER)
    return jax.shard_map(
        body, mesh=torus,
        in_specs=(split, split, P(None, OUTER), split, P(OUTER), split, split, split),
        out_specs=(split,) * 5,
        check_vma=False,
    )
```

time: 268 us -> 142 us (0.53)
  the two profiles are of different devices: /device:TPU:56 before, /device:TPU:70 now
where the time goes in v1:
time: 142 us
  Pallas kernels  140 us (99%)
  local copies, waits for them, and re-layouts  1.49 us (1%)
    pallas_call x1, Pallas kernels, body(): pl.pallas_call(transport, out_shape=(jax.ShapeDtypeStruct((count, columns...  135 us
    pallas_call x1, Pallas kernels, body(): pl.pallas_call(update, out_shape=(jax.ShapeDtypeStruct((count, columns),...  5.02 us

profile of v1, /device:TPU:70, one launch (start us, length us, event | category | flops | bytes accessed | tf_op | source)
XLA Modules:
  0.0 142.3 jit_solution(8043745717585779536)
XLA Ops:
  0.6 135.1 %transport.1 = (f32[1024,512]{1,0:T(8,128)}, f32[512,128]{1,0:T(8,128)}) custom-call(bf16[1024,512]{1,0:T(8,128)(2,1)} %tokens.1, bf16[1024,512]{1,0:T(8,128)(2,1)} %cotangent.1, bf16[4096,512]{1,0:T(8,128)(2,1)} %cache.1, bf16[128,512]{1,0:T(8,128)(2,1)} %delta.1), custom_call_target="tpu_custom_call" | custom-call | tf_op jit(solution)/shard_map/transport/pallas_call | solution.py:353
  135.8 5.0 %update.1 = (f32[1024,512]{1,0:T(8,128)}, f32[128,512]{1,0:T(8,128)}, f32[128,512]{1,0:T(8,128)}, f32[128,512]{1,0:T(8,128)}, f32[128,4]{1,0:T(8,128)}) custom-call(f32[1024,512]{1,0:T(8,128)} %get-tuple-element.7.act_in, f32[512,128]{1,0:T(8,128)} %get-tuple-element.8.grad_t, s32[1,512]{1,0:T(1,128)} %bitcast.1, f32[128,512]{1,0:T(8,128)} %master.1, ...), custom_call_target="tpu_custom_call" | custom-call | tf_op jit(solution)/shard_map/update/pallas_call | solution.py:383
  140.8 1.5 %copy.13 = f32[128,4]{0,1:T(4,128)} copy(f32[128,4]{1,0:T(8,128)} %get-tuple-element.13) | data formatting | bytes 4096 | tf_op jit(solution)/shard_map/update/pallas_call | solution.py:383

commit v2 on v1

--- a/solution.py
+++ b/solution.py
@@ -21,8 +21,8 @@
 def transport(
     tokens, cotangent, cache, delta,
     act, grad,
-    tok, cot, cot_t, weight, dbuf, gbuf, grcv, zsnd, zrcv, zloc, ysnd, yrcv,
-    load_sem, tok_send, tok_recv, d2d_send, d2d_recv, z_send, z_recv, y_send, y_recv,
+    tok, cot, cot_t, weight, dbuf, gbuf, grcv, zsnd, zmid, zrcv, zloc, ysnd, yrcv,
+    load_sem, tok_send, tok_recv, d2d_send, d2d_recv, z_send, m_recv, z_recv, y_send, y_recv,
     dy_sem, dz_send, dz_recv, dc_send, dc_recv,
 ):
     x, yh, yl = lax.axis_index("x"), lax.axis_index("yh"), lax.axis_index("yl")
@@ -47,7 +47,7 @@
     load_cot = pltpu.make_async_copy(cotangent, cot, load_sem.at[2])
     load_delta = pltpu.make_async_copy(delta, dbuf.at[z, c, yl], load_sem.at[3])
     load_cache = pltpu.make_async_copy(cache, weight, load_sem.at[4])
-    for copy in (load_a, load_b, load_cot, load_delta, load_cache):
+    for copy in (load_delta, load_a, load_b, load_cot, load_cache):
         copy.start()
 
     barrier = pltpu.get_barrier_semaphore()
@@ -87,11 +87,26 @@
         block = place // 2
         return block // 4, 2 * (block % 4) + place % 2
 
+    def offset(place):
+        return (z - target(place)[1] + NZ) % NZ
+
+    def mid_copy(place):
+        away, depth = offset(place), target(place)[1]
+        far = jnp.where(away == 4, 1, 0)
+        side = jnp.where(away == 3, 2, jnp.where(away == 5, 6, 2 + 4 * (place % 2)))
+        return pltpu.make_async_remote_copy(
+            src_ref=zsnd.at[place], dst_ref=zmid.at[place, far],
+            send_sem=z_send.at[place], recv_sem=m_recv.at[place, far],
+            device_id={"z": (depth + side) % NZ}, device_id_type=MESH,
+        )
+
     def z_copy(place):
         rows, depth = target(place)
-        return pltpu.make_async_remote_copy(
-            src_ref=zsnd.at[place], dst_ref=zrcv.at[rows, z],
-            send_sem=z_send.at[place], recv_sem=z_recv.at[rows, z],
+        away = offset(place)
+        entry = jnp.where(away < 3, away - 1, away - 4)
+        return pltpu.make_async_remote_copy(
+            src_ref=zsnd.at[place], dst_ref=zrcv.at[rows, entry],
+            send_sem=z_send.at[place], recv_sem=z_recv.at[rows, entry],
             device_id={"z": depth}, device_id_type=MESH,
         )
 
@@ -114,21 +129,56 @@
             place = pick(places, i)
             d2d_copy(place).wait_recv()
             total = gbuf[place, c] + grcv[place]
+            away = offset(place)
             zsnd[place] = total.astype(BF16)
-            rows, depth = target(place)
-
-            @pl.when(depth != z)
+
+            @pl.when((away == 1) | (away == 7))
             def _():
                 z_copy(place).start()
 
-            @pl.when(depth == z)
-            def _():
-                zloc[rows] = total
+            @pl.when((away >= 3) & (away <= 5))
+            def _():
+                mid_copy(place).start()
+
+            @pl.when((away == 2) | (away == 6))
+            def _():
+                gbuf[place, c] = total
+
+            @pl.when(away == 0)
+            def _():
+                zloc[target(place)[0]] = total
 
             return carry
 
         lax.fori_loop(0, len(places), product, 0)
         lax.fori_loop(0, len(places), merge, 0)
+
+    def relays(*places):
+        def relay(i, carry):
+            place = pick(places, i)
+            away = offset(place)
+
+            def inflow(far):
+                return pltpu.make_async_remote_copy(
+                    src_ref=zmid.at[place, far], dst_ref=zmid.at[place, far],
+                    send_sem=z_send.at[place], recv_sem=m_recv.at[place, far],
+                    device_id=up, device_id_type=MESH,
+                )
+
+            @pl.when(away == 2 + 4 * (place % 2))
+            def _():
+                inflow(1).wait_recv()
+                gbuf[place, c] += zmid[place, 1].astype(F32)
+
+            @pl.when((away == 2) | (away == 6))
+            def _():
+                inflow(0).wait_recv()
+                zsnd[place] = (gbuf[place, c] + zmid[place, 0].astype(F32)).astype(BF16)
+                z_copy(place).start()
+
+            return carry
+
+        lax.fori_loop(0, len(places), relay, 0)
 
     def dz_copy(origin, lane, peer):
         return pltpu.make_async_remote_copy(
@@ -174,6 +224,8 @@
         if 0 < step < 4:
             dc_copy(above).start()
 
+    load_delta.wait()
+    dy_copy.start()
     load_a.wait()
     send(own_a, "right")
     send(own_a, "across")
@@ -182,8 +234,6 @@
     send(own_b, "right")
     send(own_a, "left")
     send(own_b, "across")
-    load_delta.wait()
-    dy_copy.start()
     load_cot.wait()
     cot_t[...] = cot[...].T
     gradients(own_a, own_b)
@@ -197,29 +247,33 @@
     send(r_b, "across")
     arrived(p_a)
     send(p_a, "left")
+    delta_step(1)
     gradients(l_a, r_b, p_a)
-    delta_step(1)
+    relays(own_a, own_b)
 
     arrived(l_b)
     arrived(r_a)
     arrived(p_b)
+    delta_step(2)
     gradients(l_b, r_a, p_b)
-    delta_step(2)
+    relays(l_a, r_b, p_a)
 
     arrived(pl_a)
     send(pl_a, "right")
     send(p_b, "right")
     arrived(ll_a)
     arrived(ll_b)
+    delta_step(3)
     gradients(ll_a, ll_b, pl_a)
-    delta_step(3)
+    relays(l_b, r_a, p_b)
 
     arrived(pr_b)
     send(pr_b, "left")
     arrived(pr_a)
     arrived(pll_a)
+    delta_step(4)
     gradients(pr_a, pr_b, pll_a)
-    delta_step(4)
+    relays(ll_a, ll_b, pl_a)
 
     load_cache.wait()
     for origin in range(NZ):
@@ -236,33 +290,39 @@
         return carry
 
     lax.fori_loop(0, 32, rebuild, 0)
+    act[...] = jnp.zeros_like(act)
+
+    def project(*firsts):
+        def add(i, carry):
+            place = pick(firsts, i)
+            first = pl.ds(pl.multiple_of(place * HALF, HALF), HALF)
+            second = pl.ds(pl.multiple_of((place + 1) * HALF, HALF), HALF)
+            terms = jnp.dot(tok[place], weight[first, :], preferred_element_type=F32)
+            terms += jnp.dot(tok[place + 1], weight[second, :], preferred_element_type=F32)
+            act[...] += terms
+            return carry
+
+        lax.fori_loop(0, len(firsts), add, 0)
+
+    project(own_a, l_a, r_a, p_a)
+    relays(pr_a, pr_b, pll_a)
 
     arrived(pl_b)
     arrived(pll_b)
     gradients(pl_b, pll_b)
-
-    act[...] = jnp.zeros_like(act)
-
-    def project(k, carry):
-        first = pl.ds(pl.multiple_of(2 * k * HALF, HALF), HALF)
-        second = pl.ds(pl.multiple_of((2 * k + 1) * HALF, HALF), HALF)
-        terms = jnp.dot(tok[2 * k], weight[first, :], preferred_element_type=F32)
-        terms += jnp.dot(tok[2 * k + 1], weight[second, :], preferred_element_type=F32)
-        act[...] += terms
-        return carry
-
-    lax.fori_loop(0, 8, project, 0)
+    project(ll_a, pr_a)
+    relays(pl_b, pll_b)
+    project(pl_a, pll_a)
 
     def collected(rows):
         total = zloc[rows]
-        for step in range(1, NZ):
-            source = (z + step) % NZ
+        for entry in range(4):
             pltpu.make_async_remote_copy(
-                src_ref=zrcv.at[rows, source], dst_ref=zrcv.at[rows, source],
-                send_sem=z_send.at[0], recv_sem=z_recv.at[rows, source],
-                device_id={"z": source}, device_id_type=MESH,
+                src_ref=zrcv.at[rows, entry], dst_ref=zrcv.at[rows, entry],
+                send_sem=z_send.at[0], recv_sem=z_recv.at[rows, entry],
+                device_id=up, device_id_type=MESH,
             ).wait_recv()
-            total = total + zrcv[rows, source].astype(F32)
+            total = total + zrcv[rows, entry].astype(F32)
         return total
 
     ysnd[...] = collected(1 - yl).astype(BF16)
@@ -289,9 +349,13 @@
     def drain(place, carry):
         d2d_copy(place).wait_send()
 
-        @pl.when(target(place)[1] != z)
+        @pl.when(offset(place) != 0)
         def _():
-            z_copy(place).wait_send()
+            pltpu.make_async_remote_copy(
+                src_ref=zsnd.at[place], dst_ref=zmid.at[place, 0],
+                send_sem=z_send.at[place], recv_sem=m_recv.at[place, 0],
+                device_id=up, device_id_type=MESH,
+            ).wait_send()
 
         return carry
 
@@ -328,7 +392,7 @@
         smoothed = jnp.dot(
             gradient * signs, table, precision=lax.Precision.HIGHEST, preferred_element_type=F32
         )
-        scales[:, pl.ds(k, 1)] = jnp.max(jnp.abs(smoothed), axis=1, keepdims=True)
+        scales[pl.ds(k, 1), :] = jnp.max(jnp.abs(smoothed.T), axis=0, keepdims=True)
         restored = signs * jnp.dot(
             smoothed, table, precision=lax.Precision.HIGHEST, preferred_element_type=F32
         )
@@ -367,12 +431,13 @@
             pltpu.VMEM((16, 2, *piece), F32),
             pltpu.VMEM((16, *piece), F32),
             pltpu.VMEM((16, *piece), BF16),
-            pltpu.VMEM((2, NZ, *piece), BF16),
+            pltpu.VMEM((16, 2, *piece), BF16),
+            pltpu.VMEM((2, 4, *piece), BF16),
             pltpu.VMEM((2, *piece), F32),
             pltpu.VMEM(piece, BF16),
             pltpu.VMEM(piece, BF16),
             dma((5,)), dma((3, 16)), dma((16,)), dma((16,)), dma((16,)), dma((16,)),
-            dma((2, NZ)), dma, dma, dma((2,)), dma((2, NZ)), dma((NZ,)), dma((NZ,)), dma((NZ,)),
+            dma((16, 2)), dma((2, 4)), dma, dma, dma((2,)), dma((2, NZ)), dma((NZ,)), dma((NZ,)), dma((NZ,)),
         ],
         compiler_params=pltpu.CompilerParams(
             collective_id=0, has_side_effects=True, vmem_limit_bytes=58 * 2**20
@@ -385,14 +450,14 @@
         out_shape=(
             jax.ShapeDtypeStruct((count, columns), F32),
             small, small, small,
-            jax.ShapeDtypeStruct((master.shape[0], columns // BLOCK), F32),
+            jax.ShapeDtypeStruct((columns // BLOCK, master.shape[0]), F32),
         ),
         in_specs=[outside] + [inside] * 5,
         out_specs=(outside, inside, inside, inside, inside),
         scratch_shapes=[pltpu.VMEM((count, columns), F32), dma((2,))],
         name="update",
     )(act, grad_t, sign_bits.reshape(1, columns), master, moment, variance)
-    return act, new_master, new_moment, new_variance, scales
+    return act, new_master, new_moment, new_variance, scales.T
 
 
 def solution(mesh):

time: 142 us -> 103 us (0.73)
  the two profiles are of different devices: /device:TPU:70 before, /device:TPU:56 now
where the time goes in v2:
time: 103 us
  Pallas kernels  102 us (99%)
    pallas_call x1, Pallas kernels, body(): pl.pallas_call(transport, out_shape=(jax.ShapeDtypeStruct((count, columns...  97.4 us
    pallas_call x1, Pallas kernels, body(): pl.pallas_call(update, out_shape=(jax.ShapeDtypeStruct((count, columns),...  5.01 us

profile of v2, /device:TPU:56, one launch (start us, length us, event | category | flops | bytes accessed | tf_op | source)
XLA Modules:
  0.0 103.1 jit_solution(10494365101044918039)
XLA Ops:
  0.6 97.4 %transport.1 = (f32[1024,512]{1,0:T(8,128)}, f32[512,128]{1,0:T(8,128)}) custom-call(bf16[1024,512]{1,0:T(8,128)(2,1)} %tokens.1, bf16[1024,512]{1,0:T(8,128)(2,1)} %cotangent.1, bf16[4096,512]{1,0:T(8,128)(2,1)} %cache.1, bf16[128,512]{1,0:T(8,128)(2,1)} %delta.1), custom_call_target="tpu_custom_call" | custom-call | tf_op jit(solution)/shard_map/transport/pallas_call | solution.py:417
  98.0 5.0 %update.1 = (f32[1024,512]{1,0:T(8,128)}, f32[128,512]{1,0:T(8,128)}, f32[128,512]{1,0:T(8,128)}, f32[128,512]{1,0:T(8,128)}, f32[4,128]{1,0:T(4,128)}) custom-call(f32[1024,512]{1,0:T(8,128)} %get-tuple-element.12.act_in, f32[512,128]{1,0:T(8,128)} %get-tuple-element.13.grad_t, s32[1,512]{1,0:T(1,128)} %bitcast.2, f32[128,512]{1,0:T(8,128)} %master.1, ...), custom_call_target="tpu_custom_call" | custom-call | tf_op jit(solution)/shard_map/update/pallas_call | solution.py:448

commit v3 on v2

v3 whole, which is shorter than its diff:
```python
import functools

import jax
import jax.numpy as jnp
import numpy as np
from jax import lax
from jax.experimental import pallas as pl
from jax.experimental.pallas import tpu as pltpu
from jax.sharding import Mesh
from jax.sharding import PartitionSpec as P

BLOCK = 128
OUTER = ("x", "yh")
INNER = ("yl", "z", "c")
NX, NZ = 4, 8
HALF = 256
MESH = pl.DeviceIdType.MESH
F32, BF16 = jnp.float32, jnp.bfloat16


def transport(
    tokens, cotangent, cache, delta,
    act_out, grad_out,
    act, grad, tok, cot, cot_t, weight, dbuf, gbuf, grcv, zsnd, zmid, zrcv, zloc, ysnd, yrcv,
    load_sem, tok_send, tok_recv, d2d_send, d2d_recv, z_send, m_recv, z_recv, y_send, y_recv,
    dy_sem, dz_send, dz_recv, dc_send, dc_recv,
):
    x, yh, yl = lax.axis_index("x"), lax.axis_index("yh"), lax.axis_index("yl")
    z, c = lax.axis_index("z"), lax.axis_index("c")
    right, left = {"x": (x + 1) % NX}, {"x": (x + 3) % NX}
    across, beside, sibling = {"yh": 1 - yh}, {"yl": 1 - yl}, {"c": 1 - c}
    up, down = {"z": (z + 1) % NZ}, {"z": (z + 7) % NZ}

    def slot(dx, dy, half):
        row = yh if dy == 0 else 1 - yh
        return 4 * ((x + dx) % NX) + 2 * row + half

    own_a, own_b = slot(0, 0, 0), slot(0, 0, 1)
    l_a, l_b, r_a, r_b = slot(3, 0, 0), slot(3, 0, 1), slot(1, 0, 0), slot(1, 0, 1)
    ll_a, ll_b = slot(2, 0, 0), slot(2, 0, 1)
    p_a, p_b = slot(0, 1, 0), slot(0, 1, 1)
    pl_a, pl_b, pr_a, pr_b = slot(3, 1, 0), slot(3, 1, 1), slot(1, 1, 0), slot(1, 1, 1)
    pll_a, pll_b = slot(2, 1, 0), slot(2, 1, 1)

    loads = [
        pltpu.make_async_copy(
            tokens.at[:, pl.ds(BLOCK * k, BLOCK)], tok.at[2 * own_a + k], load_sem.at[k]
        )
        for k in range(4)
    ]
    load_cot = pltpu.make_async_copy(cotangent, cot, load_sem.at[4])
    load_delta = pltpu.make_async_copy(delta, dbuf.at[z, c, yl], load_sem.at[5])
    load_cache = pltpu.make_async_copy(cache, weight, load_sem.at[6])
    for copy in (load_delta, *loads, load_cot, load_cache):
        copy.start()

    barrier = pltpu.get_barrier_semaphore()
    peers = [right, left, across, beside, sibling]
    peers += [{"z": (z + step) % NZ} for step in range(1, NZ)]
    for peer in peers:
        pl.semaphore_signal(barrier, inc=1, device_id=peer, device_id_type=MESH)
    pl.semaphore_wait(barrier, len(peers))

    way = {"right": (0, right), "left": (1, left), "across": (2, across)}

    def token_copy(place, direction, part=None):
        lane, peer = way[direction]
        first = 2 * place if part is None else 2 * place + part
        piece = pl.ds(first, 2 if part is None else 1)
        return pltpu.make_async_remote_copy(
            src_ref=tok.at[piece], dst_ref=tok.at[piece],
            send_sem=tok_send.at[lane], recv_sem=tok_recv.at[first],
            device_id=peer, device_id_type=MESH,
        )

    def send(place, direction, part=None):
        token_copy(place, direction, part).start()

    def arrived(place, part=None):
        token_copy(place, "right", part).wait_recv()

    def d2d_copy(place):
        return pltpu.make_async_remote_copy(
            src_ref=gbuf.at[place, 1 - c], dst_ref=grcv.at[place],
            send_sem=d2d_send, recv_sem=d2d_recv.at[place],
            device_id=sibling, device_id_type=MESH,
        )

    def target(place):
        block = place // 2
        return block // 4, 2 * (block % 4) + place % 2

    def offset(place):
        return (z - target(place)[1] + NZ) % NZ

    def mid_copy(place):
        away, depth = offset(place), target(place)[1]
        far = jnp.where(away == 4, 1, 0)
        side = jnp.where(away == 3, 2, jnp.where(away == 5, 6, 2 + 4 * (place % 2)))
        return pltpu.make_async_remote_copy(
            src_ref=zsnd.at[place], dst_ref=zmid.at[place, far],
            send_sem=z_send, recv_sem=m_recv.at[place, far],
            device_id={"z": (depth + side) % NZ}, device_id_type=MESH,
        )

    def z_copy(place):
        rows, depth = target(place)
        away = offset(place)
        entry = jnp.where(away < 3, away - 1, away - 4)
        return pltpu.make_async_remote_copy(
            src_ref=zsnd.at[place], dst_ref=zrcv.at[rows, entry],
            send_sem=z_send, recv_sem=z_recv.at[rows, entry],
            device_id={"z": depth}, device_id_type=MESH,
        )

    def pick(places, i):
        value = places[0]
        for k in range(1, len(places)):
            value = jnp.where(i == k, places[k], value)
        return value

    def merge(place):
        d2d_copy(place).wait_recv()
        total = gbuf[place, c] + grcv[place]
        away = offset(place)
        zsnd[place] = total.astype(BF16)

        @pl.when((away == 1) | (away == 7))
        def _():
            z_copy(place).start()

        @pl.when((away >= 3) & (away <= 5))
        def _():
            mid_copy(place).start()

        @pl.when((away == 2) | (away == 6))
        def _():
            gbuf[place, c] = total

        @pl.when(away == 0)
        def _():
            zloc[target(place)[0]] = total

    def gradients(*places):
        def product(i, carry):
            place = pick(places, i)
            both = jnp.concatenate([tok[2 * place], tok[2 * place + 1]], axis=1)
            terms = jnp.dot(cot_t[...], both, preferred_element_type=F32)
            gbuf[place, 0] = terms[:, :BLOCK]
            gbuf[place, 1] = terms[:, BLOCK:]
            d2d_copy(place).start()
            return carry

        def finish(i, carry):
            merge(pick(places, i))
            return carry

        lax.fori_loop(0, len(places), product, 0)
        lax.fori_loop(0, len(places), finish, 0)

    def quarters(part, *places):
        def product(i, carry):
            place = pick(places, i)
            terms = jnp.dot(cot_t[...], tok[2 * place + part], preferred_element_type=F32)
            gbuf[place, part] = terms

            @pl.when(c != part)
            def _():
                d2d_copy(place).start()

            return carry

        def finish(i, carry):
            @pl.when(c == part)
            def _():
                merge(pick(places, i))

            return carry

        lax.fori_loop(0, len(places), product, 0)
        lax.fori_loop(0, len(places), finish, 0)

    def relays(*places):
        def relay(i, carry):
            place = pick(places, i)
            away = offset(place)

            def inflow(far):
                return pltpu.make_async_remote_copy(
                    src_ref=zmid.at[place, far], dst_ref=zmid.at[place, far],
                    send_sem=z_send, recv_sem=m_recv.at[place, far],
                    device_id=up, device_id_type=MESH,
                )

            @pl.when(away == 2 + 4 * (place % 2))
            def _():
                inflow(1).wait_recv()
                gbuf[place, c] += zmid[place, 1].astype(F32)

            @pl.when((away == 2) | (away == 6))
            def _():
                inflow(0).wait_recv()
                zsnd[place] = (gbuf[place, c] + zmid[place, 0].astype(F32)).astype(BF16)
                z_copy(place).start()

            return carry

        lax.fori_loop(0, len(places), relay, 0)

    def dz_copy(origin, peer):
        return pltpu.make_async_remote_copy(
            src_ref=dbuf.at[origin, c], dst_ref=dbuf.at[origin, c],
            send_sem=dz_send, recv_sem=dz_recv.at[origin],
            device_id=peer, device_id_type=MESH,
        )

    def dc_copy(origin):
        return pltpu.make_async_remote_copy(
            src_ref=dbuf.at[origin, c], dst_ref=dbuf.at[origin, c],
            send_sem=dc_send, recv_sem=dc_recv,
            device_id=sibling, device_id_type=MESH,
        )

    dy_copy = pltpu.make_async_remote_copy(
        src_ref=dbuf.at[z, c, yl], dst_ref=dbuf.at[z, c, yl],
        send_sem=dy_sem.at[0], recv_sem=dy_sem.at[1],
        device_id=beside, device_id_type=MESH,
    )
    dy_in = pltpu.make_async_remote_copy(
        src_ref=dbuf.at[z, c, 1 - yl], dst_ref=dbuf.at[z, c, 1 - yl],
        send_sem=dy_sem.at[0], recv_sem=dy_sem.at[1],
        device_id=beside, device_id_type=MESH,
    )

    def delta_step(step):
        below, above = (z + NZ - step) % NZ, (z + step) % NZ
        if step == 0:
            dy_in.wait_recv()
        else:
            dz_copy(below, up).wait_recv()
        if step < 4:
            dz_copy(below, up).start()
        dc_copy(below).start()
        if 0 < step < 4:
            dz_copy(above, down).wait_recv()
        if step < 3:
            dz_copy(above, down).start()
        if 0 < step < 4:
            dc_copy(above).start()

    def rebuild(j, carry):
        rows = pl.ds(pl.multiple_of(j * BLOCK, BLOCK), BLOCK)
        change = dbuf[(j % 16) // 2, j % 2, j // 16]
        weight[rows, :] = (weight[rows, :].astype(F32) + change.astype(F32)).astype(BF16)
        return carry

    def project(*firsts):
        def add(i, carry):
            first = pick(firsts, i)
            rows = pl.ds(pl.multiple_of(first * HALF, HALF), 2 * HALF)
            block = jnp.concatenate([tok[2 * first + k] for k in range(4)], axis=1)
            act[...] += jnp.dot(block, weight[rows, :], preferred_element_type=F32)
            return carry

        lax.fori_loop(0, len(firsts), add, 0)

    load_delta.wait()
    dy_copy.start()
    loads[0].wait()
    loads[1].wait()
    send(own_a, "right")
    send(own_a, "across")
    loads[2].wait()
    loads[3].wait()
    send(own_b, "left")
    send(own_b, "right")
    send(own_a, "left")
    load_cot.wait()
    cot_t[...] = cot[...].T
    gradients(own_a, own_b)
    delta_step(0)
    act[...] = jnp.zeros_like(act)

    arrived(l_a)
    send(l_a, "right")
    send(l_a, "across")
    send(own_b, "across")
    arrived(r_b)
    send(r_b, "left")
    send(r_b, "across", 0)
    send(r_b, "across", 1)
    arrived(p_a)
    send(p_a, "left")
    delta_step(1)
    gradients(l_a, r_b, p_a)
    relays(own_a, own_b)

    arrived(l_b)
    arrived(r_a)
    arrived(pl_a)
    send(pl_a, "right")
    delta_step(2)
    gradients(l_b, r_a, pl_a)
    relays(l_a, r_b, p_a)

    arrived(ll_a)
    arrived(ll_b)
    arrived(p_b)
    send(p_b, "right", 0)
    send(p_b, "right", 1)
    delta_step(3)
    gradients(ll_a, ll_b, p_b)
    relays(l_b, r_a, pl_a)

    arrived(pr_b, 0)
    send(pr_b, "left", 0)
    arrived(pr_b, 1)
    send(pr_b, "left", 1)
    relays(ll_a, ll_b, p_b)
    delta_step(4)
    arrived(pr_a)
    arrived(pll_a)
    gradients(pr_a, pr_b, pll_a)

    arrived(pl_b, 0)
    arrived(pll_b, 0)
    quarters(0, pl_b, pll_b)
    load_cache.wait()
    pltpu.make_async_remote_copy(
        src_ref=dbuf.at[:, 1 - c], dst_ref=dbuf.at[:, 1 - c],
        send_sem=dc_send, recv_sem=dc_recv,
        device_id=sibling, device_id_type=MESH,
    ).wait_recv()
    lax.fori_loop(0, 32, rebuild, 0)
    arrived(pl_b, 1)
    arrived(pll_b, 1)
    quarters(1, pl_b, pll_b)
    relays(pr_a, pr_b, pll_a)
    project(own_a, l_a, r_a)
    relays(pl_b, pll_b)
    project(p_a, ll_a, pr_a, pl_a, pll_a)
    store_act = pltpu.make_async_copy(act, act_out, load_sem.at[7])
    store_act.start()

    def collected(rows):
        total = zloc[rows]
        for entry in range(4):
            pltpu.make_async_remote_copy(
                src_ref=zrcv.at[rows, entry], dst_ref=zrcv.at[rows, entry],
                send_sem=z_send, recv_sem=z_recv.at[rows, entry],
                device_id=up, device_id_type=MESH,
            ).wait_recv()
            total = total + zrcv[rows, entry].astype(F32)
        return total

    ysnd[...] = collected(1 - yl).astype(BF16)
    y_copy = pltpu.make_async_remote_copy(
        src_ref=ysnd, dst_ref=yrcv, send_sem=y_send, recv_sem=y_recv,
        device_id=beside, device_id_type=MESH,
    )
    y_copy.start()
    grad[...] = collected(yl)
    y_copy.wait_recv()
    grad[...] += yrcv[...].astype(F32)
    store_grad = pltpu.make_async_copy(grad, grad_out, load_sem.at[8])
    store_grad.start()

    y_copy.wait_send()
    dy_copy.wait_send()
    def sent(block, sem):
        pltpu.make_async_remote_copy(
            src_ref=block, dst_ref=block, send_sem=sem, recv_sem=y_recv,
            device_id=beside, device_id_type=MESH,
        ).wait_send()

    sent(tok.at[pl.ds(0, 10)], tok_send.at[0])
    sent(tok.at[pl.ds(0, 10)], tok_send.at[1])
    sent(tok.at[pl.ds(0, 8)], tok_send.at[2])
    sent(dbuf.at[pl.ds(0, 7), c], dz_send)
    sent(dbuf.at[:, c], dc_send)
    sent(grcv, d2d_send)
    sent(zsnd.at[pl.ds(0, 14)], z_send)
    store_act.wait()
    store_grad.wait()


def hadamard(length):
    first = lax.broadcasted_iota(jnp.int32, (length, length), 0)
    second = lax.broadcasted_iota(jnp.int32, (length, length), 1)
    common = jnp.bitwise_and(first, second)
    parity = jnp.zeros((length, length), jnp.int32)
    for place in range(length.bit_length() - 1):
        parity = parity + jnp.bitwise_and(jnp.right_shift(common, place), 1)
    signs = (1 - 2 * jnp.bitwise_and(parity, 1)).astype(F32)
    return signs / np.sqrt(np.float32(length))


def update(
    act_in, grad_t, sign_bits, master, moment, variance,
    act, new_master, new_moment, new_variance, scales,
    held, grad, bits, old, out, peaks, sem_in, sem_held, sem_out,
):
    pieces = 4
    rows = held.shape[0] // pieces
    spans = [pl.ds(k * rows, rows) for k in range(pieces)]
    fetches = [
        pltpu.make_async_copy(source, target, sem_in.at[k])
        for k, (source, target) in enumerate((
            (grad_t, grad), (sign_bits, bits), (master, old.at[0]), (moment, old.at[1]), (variance, old.at[2])
        ))
    ]
    moves = [
        (
            pltpu.make_async_copy(act_in.at[span], held.at[span], sem_held.at[0, k]),
            pltpu.make_async_copy(held.at[span], act.at[span], sem_held.at[1, k]),
        )
        for k, span in enumerate(spans)
    ]
    for copy in fetches:
        copy.start()
    for fetch, _ in moves:
        fetch.start()
    table = hadamard(BLOCK)
    for copy in fetches:
        copy.wait()
    for fetch, store in moves:
        fetch.wait()
        store.start()
    for k in range(old.shape[2] // BLOCK):
        span = pl.ds(k * BLOCK, BLOCK)
        signs = (1 - 2 * bits[:, span]).astype(F32)
        gradient = grad[span, :].T
        smoothed = jnp.dot(
            gradient * signs, table, precision=lax.Precision.HIGHEST, preferred_element_type=F32
        )
        peaks[pl.ds(k, 1), :] = jnp.max(jnp.abs(smoothed.T), axis=0, keepdims=True)
        restored = signs * jnp.dot(
            smoothed, table, precision=lax.Precision.HIGHEST, preferred_element_type=F32
        )
        first = 0.9 * old[1, :, span] + 0.1 * restored
        second = 0.95 * old[2, :, span] + 0.05 * restored * restored
        corrected = first / (1.0 - 0.9**10)
        spread = jnp.sqrt(second / (1.0 - 0.95**10)) + 1e-08
        weight = old[0, :, span]
        out[0, :, span] = weight - 0.01 * (corrected / spread + 0.1 * weight)
        out[1, :, span] = first
        out[2, :, span] = second
    stores = [
        pltpu.make_async_copy(out.at[k], target, sem_out.at[k])
        for k, target in enumerate((new_master, new_moment, new_variance))
    ]
    stores.append(pltpu.make_async_copy(peaks, scales, sem_out.at[3]))
    for copy in stores:
        copy.start()
    for _, store in moves:
        store.wait()
    for copy in stores:
        copy.wait()


def body(tokens, cotangent, weight_cache, weight_delta, sign_bits, master, moment, variance):
    count, width = tokens.shape
    columns = cotangent.shape[1]
    inside = pl.BlockSpec(memory_space=pltpu.VMEM)
    outside = pl.BlockSpec(memory_space=pltpu.HBM)
    dma = pltpu.SemaphoreType.DMA
    piece = (columns, BLOCK)
    act, grad_t = pl.pallas_call(
        transport,
        out_shape=(
            jax.ShapeDtypeStruct((count, columns), F32),
            jax.ShapeDtypeStruct(piece, F32),
        ),
        in_specs=[outside] * 4,
        out_specs=(outside, outside),
        scratch_shapes=[
            pltpu.VMEM((count, columns), F32),
            pltpu.VMEM(piece, F32),
            pltpu.VMEM((32, count, BLOCK), BF16),
            pltpu.VMEM((count, columns), BF16),
            pltpu.VMEM((columns, count), BF16),
            pltpu.VMEM(weight_cache.shape, BF16),
            pltpu.VMEM((NZ, 2, 2, BLOCK, columns), BF16),
            pltpu.VMEM((16, 2, *piece), F32),
            pltpu.VMEM((16, *piece), F32),
            pltpu.VMEM((16, *piece), BF16),
            pltpu.VMEM((16, 2, *piece), BF16),
            pltpu.VMEM((2, 4, *piece), BF16),
            pltpu.VMEM((2, *piece), F32),
            pltpu.VMEM(piece, BF16),
            pltpu.VMEM(piece, BF16),
            dma((9,)), dma((3,)), dma((32,)), dma, dma((16,)), dma,
            dma((16, 2)), dma((2, 4)), dma, dma, dma((2,)), dma, dma((NZ,)), dma, dma,
        ],
        compiler_params=pltpu.CompilerParams(
            collective_id=0, has_side_effects=True, vmem_limit_bytes=58 * 2**20
        ),
        name="transport",
    )(tokens, cotangent, weight_cache, weight_delta)
    small = jax.ShapeDtypeStruct(master.shape, F32)
    act, new_master, new_moment, new_variance, scales = pl.pallas_call(
        update,
        out_shape=(
            jax.ShapeDtypeStruct((count, columns), F32),
            small, small, small,
            jax.ShapeDtypeStruct((columns // BLOCK, master.shape[0]), F32),
        ),
        in_specs=[outside] * 6,
        out_specs=(outside,) * 5,
        scratch_shapes=[
            pltpu.VMEM((count, columns), F32),
            pltpu.VMEM(piece, F32),
            pltpu.VMEM((1, columns), jnp.int32),
            pltpu.VMEM((3, *master.shape), F32),
            pltpu.VMEM((3, *master.shape), F32),
            pltpu.VMEM((columns // BLOCK, master.shape[0]), F32),
            dma((5,)), dma((2, 4)), dma((4,)),
        ],
        name="update",
    )(act, grad_t, sign_bits.reshape(1, columns), master, moment, variance)
    return act, new_master, new_moment, new_variance, scales.T


def solution(mesh):
    torus = Mesh(mesh.devices.reshape(NX, 2, 2, NZ, 2), OUTER + INNER)
    split = P(INNER, OUTER)
    return jax.shard_map(
        body, mesh=torus,
        in_specs=(split, split, P(None, OUTER), split, P(OUTER), split, split, split),
        out_specs=(split,) * 5,
        check_vma=False,
    )
```

time: 103 us -> 95.3 us (0.925)
  the two profiles are of different devices: /device:TPU:56 before, /device:TPU:232 now
where the time goes in v3:
time: 95.3 us; the launch traced here: 95.2 us
  Pallas kernels  94.6 us (99%)
    pallas_call x1, Pallas kernels, body(): pl.pallas_call(transport, out_shape=(jax.ShapeDtypeStruct((count, columns...  90.8 us
    pallas_call x1, Pallas kernels, body(): pl.pallas_call(update, out_shape=(jax.ShapeDtypeStruct((count, columns),...  3.79 us

profile of v3, /device:TPU:232, one launch (start us, length us, event | category | flops | bytes accessed | tf_op | source)
XLA Modules:
  0.0 95.2 jit_solution(3419582359913907743)
XLA Ops:
  0.6 90.8 %transport.1 = (f32[1024,512]{1,0:T(8,128)}, f32[512,128]{1,0:T(8,128)}) custom-call(bf16[1024,512]{1,0:T(8,128)(2,1)} %tokens.1, bf16[1024,512]{1,0:T(8,128)(2,1)} %cotangent.1, bf16[4096,512]{1,0:T(8,128)(2,1)} %cache.1, bf16[128,512]{1,0:T(8,128)(2,1)} %delta.1), custom_call_target="tpu_custom_call" | custom-call | tf_op jit(solution)/shard_map/transport/pallas_call | solution.py:468
  91.4 3.8 %update.1 = (f32[1024,512]{1,0:T(8,128)}, f32[128,512]{1,0:T(8,128)}, f32[128,512]{1,0:T(8,128)}, f32[128,512]{1,0:T(8,128)}, f32[4,128]{1,0:T(4,128)}) custom-call(f32[1024,512]{1,0:T(8,128)} %get-tuple-element.12.act_in, f32[512,128]{1,0:T(8,128)} %get-tuple-element.13.grad_t, s32[1,512]{1,0:T(1,128)} %bitcast.2, f32[128,512]{1,0:T(8,128)} %master.1, ...), custom_call_target="tpu_custom_call" | custom-call | tf_op jit(solution)/shard_map/update/pallas_call | solution.py:501

commit v4 on v3

--- a/solution.py
+++ b/solution.py
@@ -21,9 +21,9 @@
 def transport(
     tokens, cotangent, cache, delta,
     act_out, grad_out,
-    act, grad, tok, cot, cot_t, weight, dbuf, gbuf, grcv, zsnd, zmid, zrcv, zloc, ysnd, yrcv,
+    act, grad, tok, cot, cot_t, weight, dbuf, gbuf, grcv, zsnd, zmid, zrcv, zloc, ysnd, yrcv, yin,
     load_sem, tok_send, tok_recv, d2d_send, d2d_recv, z_send, m_recv, z_recv, y_send, y_recv,
-    dy_sem, dz_send, dz_recv, dc_send, dc_recv,
+    late_send, late_recv, dy_sem, dz_send, dz_recv, dc_send, dc_recv,
 ):
     x, yh, yl = lax.axis_index("x"), lax.axis_index("yh"), lax.axis_index("yl")
     z, c = lax.axis_index("z"), lax.axis_index("c")
@@ -99,7 +99,7 @@
         side = jnp.where(away == 3, 2, jnp.where(away == 5, 6, 2 + 4 * (place % 2)))
         return pltpu.make_async_remote_copy(
             src_ref=zsnd.at[place], dst_ref=zmid.at[place, far],
-            send_sem=z_send, recv_sem=m_recv.at[place, far],
+            send_sem=z_send.at[place], recv_sem=m_recv.at[place, far],
             device_id={"z": (depth + side) % NZ}, device_id_type=MESH,
         )
 
@@ -109,7 +109,7 @@
         entry = jnp.where(away < 3, away - 1, away - 4)
         return pltpu.make_async_remote_copy(
             src_ref=zsnd.at[place], dst_ref=zrcv.at[rows, entry],
-            send_sem=z_send, recv_sem=z_recv.at[rows, entry],
+            send_sem=z_send.at[place], recv_sem=z_recv.at[rows, entry],
             device_id={"z": depth}, device_id_type=MESH,
         )
 
@@ -119,29 +119,79 @@
             value = jnp.where(i == k, places[k], value)
         return value
 
+    late = (pr_a, pr_b, pll_a, pl_b, pll_b)
+
+    def is_late(place):
+        found = place == late[0]
+        for other in late[1:]:
+            found = found | (place == other)
+        return found
+
+    def late_index(place):
+        index = 0
+        for k in range(1, len(late)):
+            index = jnp.where(place == late[k], k, index)
+        return index
+
+    def late_copy(place):
+        k = late_index(place)
+        return pltpu.make_async_remote_copy(
+            src_ref=zsnd.at[place], dst_ref=yin.at[k],
+            send_sem=late_send.at[k], recv_sem=late_recv.at[k],
+            device_id=beside, device_id_type=MESH,
+        )
+
+    def dispatch(place, total):
+        away = offset(place)
+        zsnd[place] = total.astype(BF16)
+
+        @pl.when((away == 1) | (away == 7))
+        def _():
+            z_copy(place).start()
+
+        @pl.when((away >= 3) & (away <= 5))
+        def _():
+            mid_copy(place).start()
+
+        @pl.when((away == 2) | (away == 6))
+        def _():
+            gbuf[place, c] = total
+
+        @pl.when(away == 0)
+        def _():
+            zloc[target(place)[0]] = total
+
     def merge(place):
         d2d_copy(place).wait_recv()
+        dispatch(place, gbuf[place, c] + grcv[place])
+
+    def merge_late(place):
+        d2d_copy(place).wait_recv()
         total = gbuf[place, c] + grcv[place]
-        away = offset(place)
-        zsnd[place] = total.astype(BF16)
-
-        @pl.when((away == 1) | (away == 7))
-        def _():
-            z_copy(place).start()
-
-        @pl.when((away >= 3) & (away <= 5))
-        def _():
-            mid_copy(place).start()
-
-        @pl.when((away == 2) | (away == 6))
+
+        @pl.when(target(place)[0] != yl)
+        def _():
+            zsnd[place] = total.astype(BF16)
+            late_copy(place).start()
+
+        @pl.when(target(place)[0] == yl)
         def _():
             gbuf[place, c] = total
 
-        @pl.when(away == 0)
-        def _():
-            zloc[target(place)[0]] = total
-
-    def gradients(*places):
+    def finish_late(*places):
+        def finish(i, carry):
+            place = pick(places, i)
+
+            @pl.when(target(place)[0] == yl)
+            def _():
+                late_copy(place).wait_recv()
+                dispatch(place, gbuf[place, c] + yin[late_index(place)].astype(F32))
+
+            return carry
+
+        lax.fori_loop(0, len(places), finish, 0)
+
+    def gradients(*places, combine=merge):
         def product(i, carry):
             place = pick(places, i)
             both = jnp.concatenate([tok[2 * place], tok[2 * place + 1]], axis=1)
@@ -152,7 +202,7 @@
             return carry
 
         def finish(i, carry):
-            merge(pick(places, i))
+            combine(pick(places, i))
             return carry
 
         lax.fori_loop(0, len(places), product, 0)
@@ -173,22 +223,23 @@
         def finish(i, carry):
             @pl.when(c == part)
             def _():
-                merge(pick(places, i))
+                merge_late(pick(places, i))
 
             return carry
 
         lax.fori_loop(0, len(places), product, 0)
         lax.fori_loop(0, len(places), finish, 0)
 
-    def relays(*places):
+    def relays(*places, everywhere=True):
         def relay(i, carry):
             place = pick(places, i)
-            away = offset(place)
+            here = everywhere | (target(place)[0] == yl)
+            away = jnp.where(here, offset(place), 0)
 
             def inflow(far):
                 return pltpu.make_async_remote_copy(
                     src_ref=zmid.at[place, far], dst_ref=zmid.at[place, far],
-                    send_sem=z_send, recv_sem=m_recv.at[place, far],
+                    send_sem=z_send.at[place], recv_sem=m_recv.at[place, far],
                     device_id=up, device_id_type=MESH,
                 )
 
@@ -320,7 +371,7 @@
     delta_step(4)
     arrived(pr_a)
     arrived(pll_a)
-    gradients(pr_a, pr_b, pll_a)
+    gradients(pr_a, pr_b, pll_a, combine=merge_late)
 
     arrived(pl_b, 0)
     arrived(pll_b, 0)
@@ -335,37 +386,54 @@
     arrived(pl_b, 1)
     arrived(pll_b, 1)
     quarters(1, pl_b, pll_b)
-    relays(pr_a, pr_b, pll_a)
-    project(own_a, l_a, r_a)
-    relays(pl_b, pll_b)
-    project(p_a, ll_a, pr_a, pl_a, pll_a)
-    store_act = pltpu.make_async_copy(act, act_out, load_sem.at[7])
-    store_act.start()
+    finish_late(pr_a, pr_b, pll_a)
+    project(own_a, l_a)
+    finish_late(pl_b, pll_b)
 
     def collected(rows):
         total = zloc[rows]
         for entry in range(4):
             pltpu.make_async_remote_copy(
                 src_ref=zrcv.at[rows, entry], dst_ref=zrcv.at[rows, entry],
-                send_sem=z_send, recv_sem=z_recv.at[rows, entry],
+                send_sem=z_send.at[0], recv_sem=z_recv.at[rows, entry],
                 device_id=up, device_id_type=MESH,
             ).wait_recv()
             total = total + zrcv[rows, entry].astype(F32)
         return total
 
-    ysnd[...] = collected(1 - yl).astype(BF16)
+    mine, other = [8 * row + z for row in (yl, 1 - yl)]
     y_copy = pltpu.make_async_remote_copy(
         src_ref=ysnd, dst_ref=yrcv, send_sem=y_send, recv_sem=y_recv,
         device_id=beside, device_id_type=MESH,
     )
-    y_copy.start()
+    early_out, early_in = jnp.logical_not(is_late(other)), jnp.logical_not(is_late(mine))
+
+    @pl.when(early_out)
+    def _():
+        ysnd[...] = collected(1 - yl).astype(BF16)
+        y_copy.start()
+
+    project(r_a, p_a)
+    relays(pr_a, pr_b, pll_a, everywhere=False)
+    relays(pl_b, pll_b, everywhere=False)
+    project(ll_a, pr_a, pl_a, pll_a)
+    store_act = pltpu.make_async_copy(act, act_out, load_sem.at[7])
+    store_act.start()
+
     grad[...] = collected(yl)
-    y_copy.wait_recv()
-    grad[...] += yrcv[...].astype(F32)
+
+    @pl.when(early_in)
+    def _():
+        y_copy.wait_recv()
+        grad[...] += yrcv[...].astype(F32)
+
     store_grad = pltpu.make_async_copy(grad, grad_out, load_sem.at[8])
     store_grad.start()
 
-    y_copy.wait_send()
+    @pl.when(early_out)
+    def _():
+        y_copy.wait_send()
+
     dy_copy.wait_send()
     def sent(block, sem):
         pltpu.make_async_remote_copy(
@@ -379,7 +447,21 @@
     sent(dbuf.at[pl.ds(0, 7), c], dz_send)
     sent(dbuf.at[:, c], dc_send)
     sent(grcv, d2d_send)
-    sent(zsnd.at[pl.ds(0, 14)], z_send)
+
+    def drain(place, carry):
+        aside = is_late(place) & (target(place)[0] != yl)
+
+        @pl.when(aside)
+        def _():
+            late_copy(place).wait_send()
+
+        @pl.when(jnp.logical_not(aside) & (offset(place) != 0))
+        def _():
+            sent(zsnd.at[place], z_send.at[place])
+
+        return carry
+
+    lax.fori_loop(0, 16, drain, 0)
     store_act.wait()
     store_grad.wait()
 
@@ -489,8 +571,9 @@
             pltpu.VMEM((2, *piece), F32),
             pltpu.VMEM(piece, BF16),
             pltpu.VMEM(piece, BF16),
-            dma((9,)), dma((3,)), dma((32,)), dma, dma((16,)), dma,
-            dma((16, 2)), dma((2, 4)), dma, dma, dma((2,)), dma, dma((NZ,)), dma, dma,
+            pltpu.VMEM((5, *piece), BF16),
+            dma((9,)), dma((3,)), dma((32,)), dma, dma((16,)), dma((16,)),
+            dma((16, 2)), dma((2, 4)), dma, dma, dma((5,)), dma((5,)), dma((2,)), dma, dma((NZ,)), dma, dma,
         ],
         compiler_params=pltpu.CompilerParams(
             collective_id=0, has_side_effects=True, vmem_limit_bytes=58 * 2**20

time: 95.3 us -> 92.8 us (0.974)
  the two profiles are of different devices: /device:TPU:232 before, /device:TPU:231 now
where the time goes in v4:
time: 92.8 us; the launch traced here: 92.7 us
  Pallas kernels  92.1 us (99%)
    pallas_call x1, Pallas kernels, body(): pl.pallas_call(transport, out_shape=(jax.ShapeDtypeStruct((count, columns...  88.3 us
    pallas_call x1, Pallas kernels, body(): pl.pallas_call(update, out_shape=(jax.ShapeDtypeStruct((count, columns),...  3.79 us

profile of v4, /device:TPU:231, one launch (start us, length us, event | category | flops | bytes accessed | tf_op | source)
XLA Modules:
  0.0 92.7 jit_solution(6861391866089015657)
XLA Ops:
  0.6 88.3 %transport.1 = (f32[1024,512]{1,0:T(8,128)}, f32[512,128]{1,0:T(8,128)}) custom-call(bf16[1024,512]{1,0:T(8,128)(2,1)} %tokens.1, bf16[1024,512]{1,0:T(8,128)(2,1)} %cotangent.1, bf16[4096,512]{1,0:T(8,128)(2,1)} %cache.1, bf16[128,512]{1,0:T(8,128)(2,1)} %delta.1), custom_call_target="tpu_custom_call" | custom-call | tf_op jit(solution)/shard_map/transport/pallas_call | solution.py:550
  88.9 3.8 %update.1 = (f32[1024,512]{1,0:T(8,128)}, f32[128,512]{1,0:T(8,128)}, f32[128,512]{1,0:T(8,128)}, f32[128,512]{1,0:T(8,128)}, f32[4,128]{1,0:T(4,128)}) custom-call(f32[1024,512]{1,0:T(8,128)} %get-tuple-element.12.act_in, f32[512,128]{1,0:T(8,128)} %get-tuple-element.13.grad_t, s32[1,512]{1,0:T(1,128)} %bitcast.2, f32[128,512]{1,0:T(8,128)} %master.1, ...), custom_call_target="tpu_custom_call" | custom-call | tf_op jit(solution)/shard_map/update/pallas_call | solution.py:584

commit v5 on v4

--- a/solution.py
+++ b/solution.py
@@ -94,12 +94,13 @@
         return (z - target(place)[1] + NZ) % NZ
 
     def mid_copy(place):
-        away, depth = offset(place), target(place)[1]
+        away = offset(place)
+        rows, depth = target(place)
         far = jnp.where(away == 4, 1, 0)
         side = jnp.where(away == 3, 2, jnp.where(away == 5, 6, 2 + 4 * (place % 2)))
         return pltpu.make_async_remote_copy(
-            src_ref=zsnd.at[place], dst_ref=zmid.at[place, far],
-            send_sem=z_send.at[place], recv_sem=m_recv.at[place, far],
+            src_ref=zsnd.at[place], dst_ref=zmid.at[rows, side // 4, far],
+            send_sem=z_send.at[place], recv_sem=m_recv.at[rows, side // 4, far],
             device_id={"z": (depth + side) % NZ}, device_id_type=MESH,
         )
 
@@ -236,22 +237,24 @@
             here = everywhere | (target(place)[0] == yl)
             away = jnp.where(here, offset(place), 0)
 
+            rows, side = target(place)[0], away // 4
+
             def inflow(far):
                 return pltpu.make_async_remote_copy(
-                    src_ref=zmid.at[place, far], dst_ref=zmid.at[place, far],
-                    send_sem=z_send.at[place], recv_sem=m_recv.at[place, far],
+                    src_ref=zmid.at[rows, side, far], dst_ref=zmid.at[rows, side, far],
+                    send_sem=z_send.at[place], recv_sem=m_recv.at[rows, side, far],
                     device_id=up, device_id_type=MESH,
                 )
 
             @pl.when(away == 2 + 4 * (place % 2))
             def _():
                 inflow(1).wait_recv()
-                gbuf[place, c] += zmid[place, 1].astype(F32)
+                gbuf[place, c] += zmid[rows, side, 1].astype(F32)
 
             @pl.when((away == 2) | (away == 6))
             def _():
                 inflow(0).wait_recv()
-                zsnd[place] = (gbuf[place, c] + zmid[place, 0].astype(F32)).astype(BF16)
+                zsnd[place] = (gbuf[place, c] + zmid[rows, side, 0].astype(F32)).astype(BF16)
                 z_copy(place).start()
 
             return carry
@@ -365,13 +368,14 @@
 
     arrived(pr_b, 0)
     send(pr_b, "left", 0)
+    arrived(pr_a)
+    arrived(pll_a)
+    gradients(pr_a, pll_a, combine=merge_late)
     arrived(pr_b, 1)
     send(pr_b, "left", 1)
+    gradients(pr_b, combine=merge_late)
     relays(ll_a, ll_b, p_b)
     delta_step(4)
-    arrived(pr_a)
-    arrived(pll_a)
-    gradients(pr_a, pr_b, pll_a, combine=merge_late)
 
     arrived(pl_b, 0)
     arrived(pll_b, 0)
@@ -382,11 +386,12 @@
         send_sem=dc_send, recv_sem=dc_recv,
         device_id=sibling, device_id_type=MESH,
     ).wait_recv()
+    finish_late(pr_a, pll_a)
     lax.fori_loop(0, 32, rebuild, 0)
     arrived(pl_b, 1)
     arrived(pll_b, 1)
     quarters(1, pl_b, pll_b)
-    finish_late(pr_a, pr_b, pll_a)
+    finish_late(pr_b)
     project(own_a, l_a)
     finish_late(pl_b, pll_b)
 
@@ -566,14 +571,14 @@
             pltpu.VMEM((16, 2, *piece), F32),
             pltpu.VMEM((16, *piece), F32),
             pltpu.VMEM((16, *piece), BF16),
-            pltpu.VMEM((16, 2, *piece), BF16),
+            pltpu.VMEM((2, 2, 2, *piece), BF16),
             pltpu.VMEM((2, 4, *piece), BF16),
             pltpu.VMEM((2, *piece), F32),
             pltpu.VMEM(piece, BF16),
             pltpu.VMEM(piece, BF16),
             pltpu.VMEM((5, *piece), BF16),
             dma((9,)), dma((3,)), dma((32,)), dma, dma((16,)), dma((16,)),
-            dma((16, 2)), dma((2, 4)), dma, dma, dma((5,)), dma((5,)), dma((2,)), dma, dma((NZ,)), dma, dma,
+            dma((2, 2, 2)), dma((2, 4)), dma, dma, dma((5,)), dma((5,)), dma((2,)), dma, dma((NZ,)), dma, dma,
         ],
         compiler_params=pltpu.CompilerParams(
             collective_id=0, has_side_effects=True, vmem_limit_bytes=58 * 2**20

time: 92.8 us -> 89 us (0.959)
  the two profiles are of different devices: /device:TPU:231 before, /device:TPU:56 now
where the time goes in v5:
time: 89 us; the launch traced here: 87.5 us
  Pallas kernels  86.8 us (98%)
    pallas_call x1, Pallas kernels, body(): pl.pallas_call(transport, out_shape=(jax.ShapeDtypeStruct((count, columns...  83 us
    pallas_call x1, Pallas kernels, body(): pl.pallas_call(update, out_shape=(jax.ShapeDtypeStruct((count, columns),...  3.79 us

profile of v5, /device:TPU:56, one launch (start us, length us, event | category | flops | bytes accessed | tf_op | source)
XLA Modules:
  0.0 87.5 jit_solution(15316202687537410179)
XLA Ops:
  0.6 83.0 %transport.1 = (f32[1024,512]{1,0:T(8,128)}, f32[512,128]{1,0:T(8,128)}) custom-call(bf16[1024,512]{1,0:T(8,128)(2,1)} %tokens.1, bf16[1024,512]{1,0:T(8,128)(2,1)} %cotangent.1, bf16[4096,512]{1,0:T(8,128)(2,1)} %cache.1, bf16[128,512]{1,0:T(8,128)(2,1)} %delta.1), custom_call_target="tpu_custom_call" | custom-call | tf_op jit(solution)/shard_map/transport/pallas_call | solution.py:555
  83.7 3.8 %update.1 = (f32[1024,512]{1,0:T(8,128)}, f32[128,512]{1,0:T(8,128)}, f32[128,512]{1,0:T(8,128)}, f32[128,512]{1,0:T(8,128)}, f32[4,128]{1,0:T(4,128)}) custom-call(f32[1024,512]{1,0:T(8,128)} %get-tuple-element.12.act_in, f32[512,128]{1,0:T(8,128)} %get-tuple-element.13.grad_t, s32[1,512]{1,0:T(1,128)} %bitcast.2, f32[128,512]{1,0:T(8,128)} %master.1, ...), custom_call_target="tpu_custom_call" | custom-call | tf_op jit(solution)/shard_map/update/pallas_call | solution.py:589

commit v6 on v5

--- a/solution.py
+++ b/solution.py
@@ -20,8 +20,8 @@
 
 def transport(
     tokens, cotangent, cache, delta,
-    act_out, grad_out,
-    act, grad, tok, cot, cot_t, weight, dbuf, gbuf, grcv, zsnd, zmid, zrcv, zloc, ysnd, yrcv, yin,
+    act, grad,
+    tok, cot, cot_t, weight, dbuf, gbuf, grcv, zsnd, zmid, zrcv, zloc, ysnd, yrcv, yin,
     load_sem, tok_send, tok_recv, d2d_send, d2d_recv, z_send, m_recv, z_recv, y_send, y_recv,
     late_send, late_recv, dy_sem, dz_send, dz_recv, dc_send, dc_recv,
 ):
@@ -56,7 +56,7 @@
 
     barrier = pltpu.get_barrier_semaphore()
     peers = [right, left, across, beside, sibling]
-    peers += [{"z": (z + step) % NZ} for step in range(1, NZ)]
+    peers += [{"z": (z + step) % NZ} for step in (1, 2, 6, 7)]
     for peer in peers:
         pl.semaphore_signal(barrier, inc=1, device_id=peer, device_id_type=MESH)
     pl.semaphore_wait(barrier, len(peers))
@@ -212,6 +212,7 @@
     def quarters(part, *places):
         def product(i, carry):
             place = pick(places, i)
+            arrived(place, part)
             terms = jnp.dot(cot_t[...], tok[2 * place + part], preferred_element_type=F32)
             gbuf[place, part] = terms
 
@@ -377,8 +378,6 @@
     relays(ll_a, ll_b, p_b)
     delta_step(4)
 
-    arrived(pl_b, 0)
-    arrived(pll_b, 0)
     quarters(0, pl_b, pll_b)
     load_cache.wait()
     pltpu.make_async_remote_copy(
@@ -388,8 +387,6 @@
     ).wait_recv()
     finish_late(pr_a, pll_a)
     lax.fori_loop(0, 32, rebuild, 0)
-    arrived(pl_b, 1)
-    arrived(pll_b, 1)
     quarters(1, pl_b, pll_b)
     finish_late(pr_b)
     project(own_a, l_a)
@@ -418,12 +415,10 @@
         ysnd[...] = collected(1 - yl).astype(BF16)
         y_copy.start()
 
+    relays(pr_a, pr_b, pll_a, everywhere=False)
     project(r_a, p_a)
-    relays(pr_a, pr_b, pll_a, everywhere=False)
     relays(pl_b, pll_b, everywhere=False)
     project(ll_a, pr_a, pl_a, pll_a)
-    store_act = pltpu.make_async_copy(act, act_out, load_sem.at[7])
-    store_act.start()
 
     grad[...] = collected(yl)
 
@@ -432,8 +427,6 @@
         y_copy.wait_recv()
         grad[...] += yrcv[...].astype(F32)
 
-    store_grad = pltpu.make_async_copy(grad, grad_out, load_sem.at[8])
-    store_grad.start()
 
     @pl.when(early_out)
     def _():
@@ -467,8 +460,6 @@
         return carry
 
     lax.fori_loop(0, 16, drain, 0)
-    store_act.wait()
-    store_grad.wait()
 
 
 def hadamard(length):
@@ -483,37 +474,14 @@
 
 
 def update(
-    act_in, grad_t, sign_bits, master, moment, variance,
+    act_in, grad, bits, master, moment, variance,
     act, new_master, new_moment, new_variance, scales,
-    held, grad, bits, old, out, peaks, sem_in, sem_held, sem_out,
+    out, peaks, sem_act, sem_out,
 ):
-    pieces = 4
-    rows = held.shape[0] // pieces
-    spans = [pl.ds(k * rows, rows) for k in range(pieces)]
-    fetches = [
-        pltpu.make_async_copy(source, target, sem_in.at[k])
-        for k, (source, target) in enumerate((
-            (grad_t, grad), (sign_bits, bits), (master, old.at[0]), (moment, old.at[1]), (variance, old.at[2])
-        ))
-    ]
-    moves = [
-        (
-            pltpu.make_async_copy(act_in.at[span], held.at[span], sem_held.at[0, k]),
-            pltpu.make_async_copy(held.at[span], act.at[span], sem_held.at[1, k]),
-        )
-        for k, span in enumerate(spans)
-    ]
-    for copy in fetches:
-        copy.start()
-    for fetch, _ in moves:
-        fetch.start()
+    move = pltpu.make_async_copy(act_in, act, sem_act)
+    move.start()
     table = hadamard(BLOCK)
-    for copy in fetches:
-        copy.wait()
-    for fetch, store in moves:
-        fetch.wait()
-        store.start()
-    for k in range(old.shape[2] // BLOCK):
+    for k in range(master.shape[1] // BLOCK):
         span = pl.ds(k * BLOCK, BLOCK)
         signs = (1 - 2 * bits[:, span]).astype(F32)
         gradient = grad[span, :].T
@@ -524,11 +492,11 @@
         restored = signs * jnp.dot(
             smoothed, table, precision=lax.Precision.HIGHEST, preferred_element_type=F32
         )
-        first = 0.9 * old[1, :, span] + 0.1 * restored
-        second = 0.95 * old[2, :, span] + 0.05 * restored * restored
+        first = 0.9 * moment[:, span] + 0.1 * restored
+        second = 0.95 * variance[:, span] + 0.05 * restored * restored
         corrected = first / (1.0 - 0.9**10)
         spread = jnp.sqrt(second / (1.0 - 0.95**10)) + 1e-08
-        weight = old[0, :, span]
+        weight = master[:, span]
         out[0, :, span] = weight - 0.01 * (corrected / spread + 0.1 * weight)
         out[1, :, span] = first
         out[2, :, span] = second
@@ -539,8 +507,7 @@
     stores.append(pltpu.make_async_copy(peaks, scales, sem_out.at[3]))
     for copy in stores:
         copy.start()
-    for _, store in moves:
-        store.wait()
+    move.wait()
     for copy in stores:
         copy.wait()
 
@@ -559,10 +526,8 @@
             jax.ShapeDtypeStruct(piece, F32),
         ),
         in_specs=[outside] * 4,
-        out_specs=(outside, outside),
+        out_specs=(inside, inside),
         scratch_shapes=[
-            pltpu.VMEM((count, columns), F32),
-            pltpu.VMEM(piece, F32),
             pltpu.VMEM((32, count, BLOCK), BF16),
             pltpu.VMEM((count, columns), BF16),
             pltpu.VMEM((columns, count), BF16),
@@ -577,14 +542,14 @@
             pltpu.VMEM(piece, BF16),
             pltpu.VMEM(piece, BF16),
             pltpu.VMEM((5, *piece), BF16),
-            dma((9,)), dma((3,)), dma((32,)), dma, dma((16,)), dma((16,)),
+            dma((7,)), dma((3,)), dma((32,)), dma, dma((16,)), dma((16,)),
             dma((2, 2, 2)), dma((2, 4)), dma, dma, dma((5,)), dma((5,)), dma((2,)), dma, dma((NZ,)), dma, dma,
         ],
         compiler_params=pltpu.CompilerParams(
-            collective_id=0, has_side_effects=True, vmem_limit_bytes=58 * 2**20
+            collective_id=0, has_side_effects=True, vmem_limit_bytes=46 * 2**20
         ),
         name="transport",
-    )(tokens, cotangent, weight_cache, weight_delta)
+    )(*[pltpu.with_memory_space_constraint(a, pltpu.HBM) for a in (tokens, cotangent, weight_cache, weight_delta)])
     small = jax.ShapeDtypeStruct(master.shape, F32)
     act, new_master, new_moment, new_variance, scales = pl.pallas_call(
         update,
@@ -593,17 +558,14 @@
             small, small, small,
             jax.ShapeDtypeStruct((columns // BLOCK, master.shape[0]), F32),
         ),
-        in_specs=[outside] * 6,
+        in_specs=[inside] * 6,
         out_specs=(outside,) * 5,
         scratch_shapes=[
-            pltpu.VMEM((count, columns), F32),
-            pltpu.VMEM(piece, F32),
-            pltpu.VMEM((1, columns), jnp.int32),
-            pltpu.VMEM((3, *master.shape), F32),
             pltpu.VMEM((3, *master.shape), F32),
             pltpu.VMEM((columns // BLOCK, master.shape[0]), F32),
-            dma((5,)), dma((2, 4)), dma((4,)),
+            dma, dma((4,)),
         ],
+        compiler_params=pltpu.CompilerParams(vmem_limit_bytes=10 * 2**20),
         name="update",
     )(act, grad_t, sign_bits.reshape(1, columns), master, moment, variance)
     return act, new_master, new_moment, new_variance, scales.T

time: 89 us -> 86.4 us (0.971)
  Pallas kernels: 86.8 us -> 84.1 us
    pallas_call x1, Pallas kernels: 3.79 us -> 1.85 us  [body(): pl.pallas_call(update, out_shape=(jax.ShapeDtypeStruct((count, columns),...]
where the time goes in v6:
time: 86.4 us; the launch traced here: 84.9 us
  Pallas kernels  84.1 us (97%)
    pallas_call x1, Pallas kernels, body(): pl.pallas_call(transport, out_shape=(jax.ShapeDtypeStruct((count, columns...  82.3 us
    pallas_call x1, Pallas kernels, body(): pl.pallas_call(update, out_shape=(jax.ShapeDtypeStruct((count, columns),...  1.85 us

profile of v6, /device:TPU:56, one launch (start us, length us, event | category | flops | bytes accessed | tf_op | source)
XLA Modules:
  0.0 84.9 jit_solution(6644052886881004721)
XLA Ops:
  0.6 0.0 copy-start
  0.6 0.0 copy-start.1
  0.7 0.0 copy-start.2
  0.7 0.0 copy-start.3
  0.7 82.3 %transport.1 = (f32[1024,512]{1,0:T(8,128)S(1)}, f32[512,128]{1,0:T(8,128)S(1)}) custom-call(bf16[1024,512]{1,0:T(8,128)(2,1)} %tokens.1, bf16[1024,512]{1,0:T(8,128)(2,1)} %cotangent.1, bf16[4096,512]{1,0:T(8,128)(2,1)} %cache.1, bf16[128,512]{1,0:T(8,128)(2,1)} %delta.1), custom_call_target="tpu_custom_call" | custom-call | tf_op jit(solution)/shard_map/transport/pallas_call | solution.py:522
  83.0 0.0 copy-done
  83.0 0.0 copy-done.1
  83.0 0.0 copy-done.2
  83.0 0.0 copy-done.3
  83.0 1.8 %update.1 = (f32[1024,512]{1,0:T(8,128)}, f32[128,512]{1,0:T(8,128)}, f32[128,512]{1,0:T(8,128)}, f32[128,512]{1,0:T(8,128)}, f32[4,128]{1,0:T(4,128)}) custom-call(f32[1024,512]{1,0:T(8,128)S(1)} %get-tuple-element.12.act_in, f32[512,128]{1,0:T(8,128)S(1)} %get-tuple-element.13.grad, s32[1,512]{1,0:T(1,128)S(1)} %bitcast.2, f32[128,512]{1,0:T(8,128)S(1)} %copy-done, ...), custom_call_target="tpu_custom_call" | custom-call | tf_op jit(solution)/shard_map/update/pallas_call | solution.py:554
Async XLA Ops:
  0.6 82.3 %copy-start = (f32[128,512]{1,0:T(8,128)S(1)}, f32[128,512]{1,0:T(8,128)}, u32[]{:S(2)}) copy-start(f32[128,512]{1,0:T(8,128)} %master.1) | copy-start | bytes 786436
  0.6 82.3 %copy-start.1 = (f32[128,512]{1,0:T(8,128)S(1)}, f32[128,512]{1,0:T(8,128)}, u32[]{:S(2)}) copy-start(f32[128,512]{1,0:T(8,128)} %moment.1) | copy-start | bytes 786436
  0.7 82.3 %copy-start.2 = (f32[128,512]{1,0:T(8,128)S(1)}, f32[128,512]{1,0:T(8,128)}, u32[]{:S(2)}) copy-start(f32[128,512]{1,0:T(8,128)} %variance.1) | copy-start | bytes 786436
  0.7 82.3 %copy-start.3 = (s32[512]{0:T(512)S(1)}, s32[512]{0:T(512)}, u32[]{:S(2)}) copy-start(s32[512]{0:T(512)} %param.12) | copy-start | bytes 6148

commit v7 on v6

--- a/solution.py
+++ b/solution.py
@@ -209,7 +209,7 @@
         lax.fori_loop(0, len(places), product, 0)
         lax.fori_loop(0, len(places), finish, 0)
 
-    def quarters(part, *places):
+    def quarters(part, *places, between=()):
         def product(i, carry):
             place = pick(places, i)
             arrived(place, part)
@@ -230,6 +230,8 @@
             return carry
 
         lax.fori_loop(0, len(places), product, 0)
+        if between:
+            finish_late(*between)
         lax.fori_loop(0, len(places), finish, 0)
 
     def relays(*places, everywhere=True):
@@ -387,8 +389,7 @@
     ).wait_recv()
     finish_late(pr_a, pll_a)
     lax.fori_loop(0, 32, rebuild, 0)
-    quarters(1, pl_b, pll_b)
-    finish_late(pr_b)
+    quarters(1, pl_b, pll_b, between=(pr_b,))
     project(own_a, l_a)
     finish_late(pl_b, pll_b)
 
@@ -420,14 +421,6 @@
     relays(pl_b, pll_b, everywhere=False)
     project(ll_a, pr_a, pl_a, pll_a)
 
-    grad[...] = collected(yl)
-
-    @pl.when(early_in)
-    def _():
-        y_copy.wait_recv()
-        grad[...] += yrcv[...].astype(F32)
-
-
     @pl.when(early_out)
     def _():
         y_copy.wait_send()
@@ -460,6 +453,13 @@
         return carry
 
     lax.fori_loop(0, 16, drain, 0)
+
+    grad[...] = collected(yl)
+
+    @pl.when(early_in)
+    def _():
+        y_copy.wait_recv()
+        grad[...] += yrcv[...].astype(F32)
 
 
 def hadamard(length):

time: 86.4 us -> 85.9 us (level)
  no operation moved by 1% of the time
where the time goes in v7:
time: 85.9 us; the launch traced here: 84.3 us
  Pallas kernels  83.6 us (97%)
    pallas_call x1, Pallas kernels, body(): pl.pallas_call(transport, out_shape=(jax.ShapeDtypeStruct((count, columns...  81.8 us
    pallas_call x1, Pallas kernels, body(): pl.pallas_call(update, out_shape=(jax.ShapeDtypeStruct((count, columns),...  1.85 us

profile of v7, /device:TPU:56, one launch (start us, length us, event | category | flops | bytes accessed | tf_op | source)
XLA Modules:
  0.0 84.3 jit_solution(8251986919101059372)
XLA Ops:
  0.6 0.0 copy-start
  0.6 0.0 copy-start.1
  0.7 0.0 copy-start.2
  0.7 0.0 copy-start.3
  0.7 81.8 %transport.1 = (f32[1024,512]{1,0:T(8,128)S(1)}, f32[512,128]{1,0:T(8,128)S(1)}) custom-call(bf16[1024,512]{1,0:T(8,128)(2,1)} %tokens.1, bf16[1024,512]{1,0:T(8,128)(2,1)} %cotangent.1, bf16[4096,512]{1,0:T(8,128)(2,1)} %cache.1, bf16[128,512]{1,0:T(8,128)(2,1)} %delta.1), custom_call_target="tpu_custom_call" | custom-call | tf_op jit(solution)/shard_map/transport/pallas_call | solution.py:522
  82.5 0.0 copy-done
  82.5 0.0 copy-done.1
  82.5 0.0 copy-done.2
  82.5 0.0 copy-done.3
  82.5 1.8 %update.1 = (f32[1024,512]{1,0:T(8,128)}, f32[128,512]{1,0:T(8,128)}, f32[128,512]{1,0:T(8,128)}, f32[128,512]{1,0:T(8,128)}, f32[4,128]{1,0:T(4,128)}) custom-call(f32[1024,512]{1,0:T(8,128)S(1)} %get-tuple-element.12.act_in, f32[512,128]{1,0:T(8,128)S(1)} %get-tuple-element.13.grad, s32[1,512]{1,0:T(1,128)S(1)} %bitcast.2, f32[128,512]{1,0:T(8,128)S(1)} %copy-done, ...), custom_call_target="tpu_custom_call" | custom-call | tf_op jit(solution)/shard_map/update/pallas_call | solution.py:554
Async XLA Ops:
  0.6 81.8 %copy-start = (f32[128,512]{1,0:T(8,128)S(1)}, f32[128,512]{1,0:T(8,128)}, u32[]{:S(2)}) copy-start(f32[128,512]{1,0:T(8,128)} %master.1) | copy-start | bytes 786436
  0.6 81.8 %copy-start.1 = (f32[128,512]{1,0:T(8,128)S(1)}, f32[128,512]{1,0:T(8,128)}, u32[]{:S(2)}) copy-start(f32[128,512]{1,0:T(8,128)} %moment.1) | copy-start | bytes 786436
  0.7 81.8 %copy-start.2 = (f32[128,512]{1,0:T(8,128)S(1)}, f32[128,512]{1,0:T(8,128)}, u32[]{:S(2)}) copy-start(f32[128,512]{1,0:T(8,128)} %variance.1) | copy-start | bytes 786436
  0.7 81.8 %copy-start.3 = (s32[512]{0:T(512)S(1)}, s32[512]{0:T(512)}, u32[]{:S(2)}) copy-start(s32[512]{0:T(512)} %param.12) | copy-start | bytes 6148

commit v8 on v7

--- a/solution.py
+++ b/solution.py
@@ -417,9 +417,9 @@
         y_copy.start()
 
     relays(pr_a, pr_b, pll_a, everywhere=False)
-    project(r_a, p_a)
+    project(r_a)
     relays(pl_b, pll_b, everywhere=False)
-    project(ll_a, pr_a, pl_a, pll_a)
+    project(p_a, ll_a, pr_a, pl_a, pll_a)
 
     @pl.when(early_out)
     def _():

time: 85.9 us -> 85.9 us (level)
  no operation moved by 1% of the time
where the time goes in v8:
time: 85.9 us; the launch traced here: 84.3 us
  Pallas kernels  83.6 us (97%)
    pallas_call x1, Pallas kernels, body(): pl.pallas_call(transport, out_shape=(jax.ShapeDtypeStruct((count, columns...  81.8 us
    pallas_call x1, Pallas kernels, body(): pl.pallas_call(update, out_shape=(jax.ShapeDtypeStruct((count, columns),...  1.85 us

profile of v8, /device:TPU:56, one launch (start us, length us, event | category | flops | bytes accessed | tf_op | source)
XLA Modules:
  0.0 84.3 jit_solution(13537053442549188587)
XLA Ops:
  0.6 0.0 copy-start
  0.6 0.0 copy-start.1
  0.7 0.0 copy-start.2
  0.7 0.0 copy-start.3
  0.7 81.8 %transport.1 = (f32[1024,512]{1,0:T(8,128)S(1)}, f32[512,128]{1,0:T(8,128)S(1)}) custom-call(bf16[1024,512]{1,0:T(8,128)(2,1)} %tokens.1, bf16[1024,512]{1,0:T(8,128)(2,1)} %cotangent.1, bf16[4096,512]{1,0:T(8,128)(2,1)} %cache.1, bf16[128,512]{1,0:T(8,128)(2,1)} %delta.1), custom_call_target="tpu_custom_call" | custom-call | tf_op jit(solution)/shard_map/transport/pallas_call | solution.py:522
  82.5 0.0 copy-done
  82.5 0.0 copy-done.1
  82.5 0.0 copy-done.2
  82.5 0.0 copy-done.3
  82.5 1.8 %update.1 = (f32[1024,512]{1,0:T(8,128)}, f32[128,512]{1,0:T(8,128)}, f32[128,512]{1,0:T(8,128)}, f32[128,512]{1,0:T(8,128)}, f32[4,128]{1,0:T(4,128)}) custom-call(f32[1024,512]{1,0:T(8,128)S(1)} %get-tuple-element.12.act_in, f32[512,128]{1,0:T(8,128)S(1)} %get-tuple-element.13.grad, s32[1,512]{1,0:T(1,128)S(1)} %bitcast.2, f32[128,512]{1,0:T(8,128)S(1)} %copy-done, ...), custom_call_target="tpu_custom_call" | custom-call | tf_op jit(solution)/shard_map/update/pallas_call | solution.py:554
Async XLA Ops:
  0.6 81.8 %copy-start = (f32[128,512]{1,0:T(8,128)S(1)}, f32[128,512]{1,0:T(8,128)}, u32[]{:S(2)}) copy-start(f32[128,512]{1,0:T(8,128)} %master.1) | copy-start | bytes 786436
  0.6 81.8 %copy-start.1 = (f32[128,512]{1,0:T(8,128)S(1)}, f32[128,512]{1,0:T(8,128)}, u32[]{:S(2)}) copy-start(f32[128,512]{1,0:T(8,128)} %moment.1) | copy-start | bytes 786436
  0.7 81.8 %copy-start.2 = (f32[128,512]{1,0:T(8,128)S(1)}, f32[128,512]{1,0:T(8,128)}, u32[]{:S(2)}) copy-start(f32[128,512]{1,0:T(8,128)} %variance.1) | copy-start | bytes 786436
  0.7 81.8 %copy-start.3 = (s32[512]{0:T(512)S(1)}, s32[512]{0:T(512)}, u32[]{:S(2)}) copy-start(s32[512]{0:T(512)} %param.12) | copy-start | bytes 6148
